TPU v7x, 32 devices: a whole 2x2x4 slice. The times are simulated.
32 devices in a mesh: seq: 8 (over z, y), head: 4 (over x, core).
Axes of the slice: x: 2, y: 2, z: 4, core: 2. Of those that a mesh axis runs over, the one named last changes fastest.
Arguments:
- queries: bfloat16 [4096, 12288], P(('seq', 'head')), may hold values from -8 to 8
- latent: bfloat16 [4096, 512], P(('seq', 'head')), may hold values from -6 to 6
- rope_keys: bfloat16 [4096, 64], P(('seq', 'head')), may hold values from -8 to 8
- key_weight: bfloat16 [512, 8192], P('seq', 'head'), may hold values from -0.25 to 0.25
- value_weight: bfloat16 [512, 8192], P('seq', 'head'), may hold values from -0.25 to 0.25
- doc_lengths: int32 [32], replicated, may hold values from 1 to 254, as said below
Outputs:
- attended: bfloat16 [4096, 8192], P(('seq', 'head'))
Inputs may be any that keep to these rules, and one draw needn't show every extreme that they name: `doc_lengths`: the documents lie in order in the pack and their lengths sum to 4096; document 0 starts at position 0 and every other document d starts strictly inside positions d * 128 to (d + 1) * 128 - 1, excluding the first of these; one length is exactly 254.
All inputs are finite; a program needn't handle non-finite values.
Results may differ from a plain program's by a relative error of at most 0.0062.
Values may be sent and summed in bfloat16 or wider, within the bound.
A program may use at most 128 MiB of HBM per device.

v0:
```python
import functools
import math

import jax
import jax.numpy as jnp
from jax import lax
from jax.experimental import pallas as pl
from jax.experimental.pallas import tpu as pltpu
from jax.sharding import PartitionSpec as P

NOPE = 128
ROPE = 64
VDIM = 128
QK = NOPE + ROPE
LOG2E = 1.4426950408889634

MESH = pl.DeviceIdType.MESH


def kernel(
    sizes, queries, latent, rope_keys, key_weight, value_weight, lengths, out,
    lat_all, rope_all, wk, wv, qbuf, kaug, vbuf, bias, obuf,
    lat_sem, lat_send, mate_send, x_send, q_sem, q_send, w_own, w_recv, w_send, o_sem, o_send,
):
    n_seq, n_head, look, wide, chunk_heads = sizes
    tok, rank = latent.shape
    rows = key_weight.shape[0]
    half = n_seq // 2
    xs = n_head // 2
    slots = look + n_head
    span = (look + 1) * tok
    cw = chunk_heads * NOPE
    qw = chunk_heads * QK
    pieces = wide + xs
    q_all, o_all = (wide + 1) * qw, (wide + 1) * cw
    seq, head = lax.axis_index("seq"), lax.axis_index("head")
    core, x = head % 2, head // 2
    mate = head + 1 - 2 * core

    odd = seq % 2
    place = (seq // 2) * (1 - odd) + (n_seq - 1 - seq // 2) * odd

    def at_place(where):
        where = (where + n_seq) % n_seq
        fold = where // half
        return 2 * where * (1 - fold) + (2 * (n_seq - 1 - where) + 1) * fold

    after, before = at_place(place + 1), at_place(place - 1)
    next_seq, last_seq = (seq + 1) % n_seq, (seq + n_seq - 1) % n_seq

    barrier = pltpu.get_barrier_semaphore()

    def greet(to_seq, to_head):
        pl.semaphore_signal(barrier, inc=1, device_id=(to_seq, to_head), device_id_type=MESH)

    for k in range(1, n_head):
        greet(seq, (head + k) % n_head)
    greet(after, head)
    greet(before, head)
    for k in range(xs):
        greet(next_seq, ((x + k) % xs) * 2 + core)
        greet(last_seq, ((x + k) % xs) * 2 + core)

    def owner(k, side):
        return ((x + k) % xs) * 2 + side

    def q_cols(who, c):
        return pl.ds(pl.multiple_of(who * q_all + c * qw, 128), qw)

    def o_cols(who, c):
        return pl.ds(pl.multiple_of(who * o_all + c * cw, 128), cw)

    def own_copies():
        mine = look + head
        pltpu.make_async_copy(latent, lat_all.at[mine], lat_sem.at[mine, 0]).start()
        pltpu.make_async_copy(rope_keys, rope_all.at[mine], lat_sem.at[mine, 1]).start()
        for c in range(wide + 1):
            for kv, (source, held) in enumerate(((key_weight, wk), (value_weight, wv))):
                pltpu.make_async_copy(
                    source.at[:, pl.ds(c * cw, cw)], held.at[c, seq], w_own.at[c, kv]
                ).start()
        for c in range(wide):
            pltpu.make_async_copy(
                queries.at[:, q_cols(head, c)], qbuf.at[c, head], q_sem.at[c, head]
            ).start()
        for k in range(xs):
            pltpu.make_async_copy(
                queries.at[:, q_cols(owner(k, core), wide)],
                qbuf.at[wide + k, core], q_sem.at[wide + k, core],
            ).start()

    own_copies()
    pl.semaphore_wait(barrier, n_head - 1 + 2 + 2 * xs)

    def lat_copies(k, to_seq, slot):
        return [
            pltpu.make_async_remote_copy(
                src_ref=source, dst_ref=held.at[slot],
                send_sem=lat_send.at[k, part], recv_sem=lat_sem.at[slot, part],
                device_id=(to_seq, ((x + k % xs) % xs) * 2 + core), device_id_type=MESH,
            )
            for part, (source, held) in enumerate(((latent, lat_all), (rope_keys, rope_all)))
        ]

    def x_copies(k):
        return [
            pltpu.make_async_remote_copy(
                src_ref=source.at[:, pl.ds(wide * cw, cw)], dst_ref=held.at[wide + k, seq],
                send_sem=x_send.at[k - 1, kv], recv_sem=w_own.at[wide + k, kv],
                device_id=(seq, ((x + xs - k) % xs) * 2 + core), device_id_type=MESH,
            )
            for kv, (source, held) in enumerate(((key_weight, wk), (value_weight, wv)))
        ]

    def ring_parts(t):
        both = [(0, 0), (0, 1), (1, 0), (1, 1)]
        return both if t < half else [(0, 0), (1, 1)]

    def own_weights(c):
        for kv in range(2):
            mine = (wk, wv)[kv].at[c, seq]
            pltpu.make_async_copy(mine, mine, w_own.at[c, kv]).wait()

    def ring_copy(c, t, way, kv):
        origin = at_place(place - (t - 1)) if way == 0 else at_place(place + (t - 1))
        source, held = ((key_weight, wk), (value_weight, wv))[kv]
        src = source.at[:, pl.ds(c * cw, cw)] if t == 1 and c <= wide else held.at[c, origin]
        index = t - 1
        return pltpu.make_async_remote_copy(
            src_ref=src, dst_ref=held.at[c, origin],
            send_sem=w_send.at[c, index, way, kv], recv_sem=w_recv.at[c, index, way, kv],
            device_id=(after if way == 0 else before, head), device_id_type=MESH,
        )

    def ring_start(c, t):
        if c > wide:
            own_weights(c)
        for way, kv in ring_parts(t):
            ring_copy(c, t, way, kv).start()

    def ring_take(c, t):
        for way, kv in ring_parts(t):
            origin = at_place(place - t) if way == 0 else at_place(place + t)
            landed = (wk, wv)[kv].at[c, origin]
            pltpu.make_async_copy(landed, landed, w_recv.at[c, t - 1, way, kv]).wait()
            if t + 1 <= half and (way, kv) in ring_parts(t + 1):
                ring_copy(c, t + 1, way, kv).start()

    def q_copies(c):
        if c < wide:
            routes = [((head + k) % n_head,) * 2 + (head,) for k in range(1, n_head)]
        else:
            routes = [(mate, owner(c - wide, 1 - core), core)]
        return [
            pltpu.make_async_remote_copy(
                src_ref=queries.at[:, q_cols(who, min(c, wide))], dst_ref=qbuf.at[c, slot],
                send_sem=q_send.at[c, k], recv_sem=q_sem.at[c, slot],
                device_id=(seq, peer), device_id_type=MESH,
            )
            for k, (peer, who, slot) in enumerate(routes)
        ]

    def o_copies(c):
        if c < wide:
            routes = [((head + k) % n_head,) * 2 + (head, head) for k in range(1, n_head)]
        else:
            routes = [(mate, 1 - core, owner(c - wide, core), core)]
        return [
            pltpu.make_async_remote_copy(
                src_ref=obuf.at[c, tile], dst_ref=out.at[:, o_cols(who, min(c, wide))],
                send_sem=o_send.at[c, k], recv_sem=o_sem.at[c, slot],
                device_id=(seq, peer), device_id_type=MESH,
            )
            for k, (peer, tile, who, slot) in enumerate(routes)
        ]

    def o_own(c):
        if c < wide:
            tile, who, slot = head, head, head
        else:
            tile, who, slot = core, owner(c - wide, core), core
        return pltpu.make_async_copy(
            obuf.at[c, tile], out.at[:, o_cols(who, min(c, wide))], o_sem.at[c, slot]
        )

    for k in range(1, xs):
        for copy in lat_copies(k, seq, look + head):
            copy.start()

    @pl.when(head >= n_head - look)
    def _():
        for k in range(xs):
            for copy in lat_copies(xs + k, next_seq, head - (n_head - look)):
                copy.start()

    groups = [list(range(wide)), list(range(wide, pieces))]
    for c in groups[0]:
        ring_start(c, 1)
    for c in range(pieces):
        for copy in q_copies(c):
            copy.start()
        if c == 0:
            for k in range(1, xs):
                for copy in x_copies(k):
                    copy.start()

    docs = lengths.shape[0]
    first = seq * n_head * tok

    def mask_tile(j, carry):
        q_place = first + j * tok + lax.broadcasted_iota(jnp.int32, (tok, 1), 0)

        def document(d, state):
            start, begun = state
            return start + lengths[d], jnp.where(start <= q_place, start, begun)

        _, begun = lax.fori_loop(
            0, docs, document, (jnp.int32(0), jnp.zeros((tok, 1), jnp.int32)), unroll=True
        )
        k_place = first + (j - look) * tok + lax.broadcasted_iota(jnp.int32, (tok, span), 1)
        seen = (k_place >= begun) & (k_place <= q_place)
        bias[j] = jnp.where(seen, 0.0, -jnp.inf)
        return carry

    lax.fori_loop(0, n_head, mask_tile, 0)

    def lat_wait(slot):
        for part, held in enumerate((lat_all, rope_all)):
            pltpu.make_async_copy(held.at[slot], held.at[slot], lat_sem.at[slot, part]).wait()

    def mate_copies(i):
        slot = 2 * i + core
        return [
            pltpu.make_async_remote_copy(
                src_ref=held.at[slot], dst_ref=held.at[slot],
                send_sem=mate_send.at[i, part], recv_sem=lat_sem.at[slot, part],
                device_id=(seq, mate), device_id_type=MESH,
            )
            for part, held in enumerate((lat_all, rope_all))
        ]

    def lat_all_in():
        for i in list(range(look // 2, slots // 2)) + list(range(look // 2)):
            lat_wait(2 * i + core)
            for copy in mate_copies(i):
                copy.start()
        for i in range(slots // 2):
            lat_wait(2 * i + 1 - core)

    def rope_in():
        first_half = lax.broadcasted_iota(jnp.int32, (tok, 2 * ROPE), 1) < ROPE

        def fill(slot, carry):
            rope = rope_all[slot].astype(jnp.float32)
            twice = jnp.concatenate([rope, rope], axis=1)
            at = pl.ds(pl.multiple_of(slot * tok, tok), tok)
            for h in range(chunk_heads):
                shown = jnp.where(first_half, twice, 0.0) if h % 2 == 0 else twice
                kaug[h, at, NOPE:] = shown.astype(jnp.bfloat16)
            return carry

        lax.fori_loop(0, slots, fill, 0)

    block = 2 * tok

    def project(c):
        if c <= wide:
            own_weights(c)
        first_slot, blocks = (0, slots // 2) if c < wide else (2 * x, (look + 2) // 2)

        def rows_of(i, carry):
            slot = first_slot + 2 * i
            at = pl.ds(pl.multiple_of(slot * tok, tok), block)
            lat = lat_all[pl.ds(slot, 2)].reshape(block, rank)
            low = lax.broadcasted_iota(jnp.int32, (block, NOPE), 1) < ROPE
            for pair in range(chunk_heads // 2):
                cols = slice(pair * 2 * NOPE, (pair + 1) * 2 * NOPE)
                w = wk[c, :, :, cols].reshape(rank, 2 * NOPE)
                k = jnp.dot(lat, w, preferred_element_type=jnp.float32)
                kaug[2 * pair, at, :NOPE] = k[:, :NOPE].astype(jnp.bfloat16)
                turned = pltpu.roll(k[:, NOPE:], ROPE, axis=1)
                zeros_first = jnp.where(low, 0.0, turned).astype(jnp.bfloat16)
                kaug[2 * pair + 1, at, :NOPE] = zeros_first
                rope_last = kaug[2 * pair + 1, at, NOPE:].astype(jnp.float32)
                kaug[2 * pair + 1, at, NOPE:] = jnp.where(low, turned, rope_last).astype(
                    jnp.bfloat16
                )
                w = wv[c, :, :, cols].reshape(rank, 2 * VDIM)
                v = jnp.dot(lat, w, preferred_element_type=jnp.float32)
                vbuf[at, cols] = v.astype(jnp.bfloat16)
            return carry

        lax.fori_loop(0, blocks, rows_of, 0)

    scale = LOG2E / math.sqrt(QK)

    def attend(c, first_tile, last_tile):
        def tile(j, carry):
            place_of = j if c < wide else 2 * x + j
            at = pl.ds(pl.multiple_of(place_of * tok, tok), span)
            hide = bias[place_of]
            for h in range(chunk_heads):
                begin = (h // 2) * 2 * QK + (h % 2) * NOPE
                q = qbuf[c, j, :, begin:begin + 2 * NOPE]
                s = lax.dot_general(
                    q, kaug[h, at, :], (((1,), (1,)), ((), ())),
                    preferred_element_type=jnp.float32,
                )
                s = s * scale + hide
                peak = jnp.max(s, axis=1, keepdims=True)
                expo = jnp.exp2(s - peak)
                total = jnp.sum(expo, axis=1, keepdims=True)
                cols = slice(h * VDIM, (h + 1) * VDIM)
                mixed = jnp.dot(
                    expo.astype(jnp.bfloat16), vbuf[at, cols],
                    preferred_element_type=jnp.float32,
                )
                obuf[c, j, :, cols] = (mixed / total).astype(jnp.bfloat16)
            return carry

        lax.fori_loop(first_tile, last_tile, tile, 0)

    def q_in(c):
        for slot in range(n_head if c < wide else 2):
            landed = qbuf.at[c, slot]
            pltpu.make_async_copy(landed, landed, q_sem.at[c, slot]).wait()

    def give(c):
        for copy in o_copies(c):
            copy.start()
        o_own(c).start()

    def work_on(c):
        tiles = n_head if c < wide else 2

        def tiles_first():
            q_in(c)
            attend(c, 0, tiles // 2)

        def tiles_last():
            attend(c, tiles // 2, tiles)
            give(c)

        return [functools.partial(project, c), tiles_first, tiles_last]

    waiting = []
    for number, group in enumerate(groups):
        for t in range(1, half + 1):
            for c in group:
                ring_take(c, t)
                if t == half - 1 and c == group[-1] and number + 1 < len(groups):
                    for ahead in groups[number + 1]:
                        ring_start(ahead, 1)
                if number == 0 and t == 1 and c == group[-1]:
                    lat_all_in()
                    rope_in()
                if t == half:
                    waiting += work_on(c)
                for _ in range(min(1, len(waiting))):
                    waiting.pop(0)()
    for step in waiting:
        step()

    for c in range(pieces):
        for slot in range(n_head if c < wide else 2):
            who = slot if c < wide else owner(c - wide, slot)
            landed = out.at[:, o_cols(who, min(c, wide))]
            pltpu.make_async_copy(landed, landed, o_sem.at[c, slot]).wait()
        for copy in q_copies(c) + o_copies(c):
            copy.wait_send()
        for t in range(1, half + 1):
            for way, kv in ring_parts(t):
                ring_copy(c, t, way, kv).wait_send()
    for k in range(1, xs):
        for copy in lat_copies(k, seq, look + head) + x_copies(k):
            copy.wait_send()

    @pl.when(head >= n_head - look)
    def _():
        for k in range(xs):
            for copy in lat_copies(xs + k, next_seq, head - (n_head - look)):
                copy.wait_send()

    for i in range(slots // 2):
        for copy in mate_copies(i):
            copy.wait_send()


def shards(queries, latent, rope_keys, key_weight, value_weight, doc_lengths):
    n_seq, n_head = lax.axis_size("seq"), lax.axis_size("head")
    tok, rank = latent.shape
    rows = key_weight.shape[0]
    local_heads = key_weight.shape[1] // NOPE
    docs = doc_lengths.shape[0]
    slot_rows = n_seq * n_head * tok // docs
    look = 2 * -(-slot_rows // tok)
    chunk_heads = min(4, local_heads)
    wide = local_heads // chunk_heads - 1
    pieces = wide + n_head // 2
    slots, span, half = look + n_head, (look + 1) * tok, n_seq // 2
    cw, qw = chunk_heads * NOPE, chunk_heads * QK
    anywhere = pl.BlockSpec(memory_space=pl.ANY)
    dma = pltpu.SemaphoreType.DMA
    bf16 = jnp.bfloat16
    return pl.pallas_call(
        functools.partial(kernel, (n_seq, n_head, look, wide, chunk_heads)),
        out_shape=jax.ShapeDtypeStruct((tok, n_head * local_heads * VDIM), bf16),
        in_specs=[anywhere] * 5 + [pl.BlockSpec(memory_space=pltpu.SMEM)],
        out_specs=anywhere,
        scratch_shapes=[
            pltpu.VMEM((slots, tok, rank), bf16),
            pltpu.VMEM((slots, tok, ROPE), bf16),
            pltpu.VMEM((pieces, n_seq, rows, cw), bf16),
            pltpu.VMEM((pieces, n_seq, rows, cw), bf16),
            pltpu.VMEM((pieces, n_head, tok, qw), bf16),
            pltpu.VMEM((chunk_heads, slots * tok, 2 * NOPE), bf16),
            pltpu.VMEM((slots * tok, cw), bf16),
            pltpu.VMEM((n_head, tok, span), jnp.float32),
            pltpu.VMEM((pieces, n_head, tok, cw), bf16),
            dma((slots, 2)),
            dma((n_head, 2)),
            dma((slots // 2, 2)),
            dma((n_head // 2 - 1, 2)),
            dma((pieces, n_head)),
            dma((pieces, n_head - 1)),
            dma((pieces, 2)),
            dma((pieces, half, 2, 2)),
            dma((pieces, half, 2, 2)),
            dma((pieces, n_head)),
            dma((pieces, n_head - 1)),
        ],
        compiler_params=pltpu.CompilerParams(collective_id=0, has_side_effects=True),
    )(queries, latent, rope_keys, key_weight, value_weight, doc_lengths)


def solution(mesh):
    placed = (
        P(("seq", "head"), None),
        P(("seq", "head"), None),
        P(("seq", "head"), None),
        P("seq", "head"),
        P("seq", "head"),
        P(),
    )
    return jax.shard_map(
        shards, mesh=mesh, in_specs=placed, out_specs=P(("seq", "head"), None), check_vma=False
    )
```

profile of v0, /device:TPU:1, one launch (start us, length us, event | category | flops | bytes accessed | tf_op | source)
XLA Modules:
  0.0 77.3 jit_solution(13779632904228752247)
XLA Ops:
  0.0 1.4 %copy.7.rope_keys = bf16[128,64]{1,0:T(8,128)(2,1)} copy(bf16[128,64]{0,1:T(8,128)(2,1)} %param.8) | data formatting | bytes 32768 | tf_op args[2]
  1.4 72.8 %shard_map.64 = bf16[128,8192]{1,0:T(8,128)(2,1)} custom-call(bf16[128,12288]{1,0:T(8,128)(2,1)} %queries.1, bf16[128,512]{1,0:T(8,128)(2,1)} %latent.1, bf16[128,64]{1,0:T(8,128)(2,1)} %copy.7.rope_keys, bf16[64,2048]{1,0:T(8,128)(2,1)} %key_weight.1, bf16[64,2048]{1,0:T(8,128)(2,1)} %value_weight.1, s32[32]{0:T(128)} %lengths.1), custom_call_target="tpu_custom_call" | custom-call | tf_op jit(solution)/shard_map/pallas_call | solution.py:405
  74.2 3.1 %copy.9 = bf16[128,8192]{1,0:T(8,128)(2,1)} copy(bf16[128,8192]{1,0:T(8,128)(2,1)} %shard_map.64) | data formatting | bytes 4194304
where the time goes:
time: 78 us; the launch traced here: 77.3 us
  Pallas kernels  72.8 us (93%)
  local copies, waits for them, and re-layouts  4.53 us (6%)
    pallas_call x1, Pallas kernels, shards(): pl.pallas_call(functools.partial(kernel, (n_seq, n_head, look, wide, chun...  72.8 us
    unnamed x2, local copies, waits for them, and re-layouts  4.53 us

commit v1 on v0

v1 whole, which is shorter than its diff:
```python
import functools
import math

import jax
import jax.numpy as jnp
from jax import lax
from jax.experimental import pallas as pl
from jax.experimental.pallas import tpu as pltpu
from jax.sharding import PartitionSpec as P

NOPE = 128
ROPE = 64
VDIM = 128
QK = NOPE + ROPE
LOG2E = 1.4426950408889634

MESH = pl.DeviceIdType.MESH


def kernel(
    sizes, queries, latent, rope_keys, key_weight, value_weight, lengths, out,
    lat_all, rope_all, w, qbuf, kaug, vbuf, bias, obuf,
    lat_sem, lat_send, w_own, w_recv, w_send, x_send, q_sem, q_send, o_sem, o_send,
):
    n_seq, n_head, look, wide, chunk_heads = sizes
    tok, rank = latent.shape
    half = n_seq // 2
    xs = n_head // 2
    slots = look + n_head
    span = (look + 1) * tok
    cw = chunk_heads * NOPE
    qw = chunk_heads * QK
    pieces = wide + xs
    q_all, o_all = (wide + 1) * qw, (wide + 1) * cw
    seq, head = lax.axis_index("seq"), lax.axis_index("head")
    core, x = head % 2, head // 2
    mate = head + 1 - 2 * core

    odd = seq % 2
    place = (seq // 2) * (1 - odd) + (n_seq - 1 - seq // 2) * odd

    def at_place(where):
        where = (where + n_seq) % n_seq
        fold = where // half
        return 2 * where * (1 - fold) + (2 * (n_seq - 1 - where) + 1) * fold

    after, before = at_place(place + 1), at_place(place - 1)

    shown = head - (n_head - look)
    gives = (shown >= 0) & (seq < n_seq - 1)
    takes = (shown >= 0) & (seq > 0)

    barrier = pltpu.get_barrier_semaphore()

    def greet(to_seq, to_head):
        pl.semaphore_signal(barrier, inc=1, device_id=(to_seq, to_head), device_id_type=MESH)

    greet(after, head)
    greet(before, head)
    for k in range(1, n_head):
        greet(seq, (head + k) % n_head)

    @pl.when(gives)
    def _():
        greet(seq + 1, head)

    @pl.when(takes)
    def _():
        greet(seq - 1, head)

    def owner(k, side):
        return ((x + k) % xs) * 2 + side

    def q_cols(who, c):
        return pl.ds(pl.multiple_of(who * q_all + c * qw, 128), qw)

    def o_cols(who, c):
        return pl.ds(pl.multiple_of(who * o_all + c * cw, 128), cw)

    def own_copies():
        mine = look + head
        pltpu.make_async_copy(latent, lat_all.at[mine], lat_sem.at[mine, 0]).start()
        pltpu.make_async_copy(rope_keys, rope_all.at[mine], lat_sem.at[mine, 1]).start()
        for c in range(wide + 1):
            for kv, source in enumerate((key_weight, value_weight)):
                pltpu.make_async_copy(
                    source.at[:, pl.ds(c * cw, cw)], w.at[c, seq, kv], w_own.at[c]
                ).start()
        for c in range(wide):
            pltpu.make_async_copy(
                queries.at[:, q_cols(head, c)], qbuf.at[c, head], q_sem.at[c]
            ).start()
        for k in range(xs):
            pltpu.make_async_copy(
                queries.at[:, q_cols(owner(k, core), wide)],
                qbuf.at[wide + k, core], q_sem.at[wide + k],
            ).start()

    own_copies()
    with jax.named_scope("barrier"):
        pl.semaphore_wait(
            barrier, n_head + 1 + gives.astype(jnp.int32) + takes.astype(jnp.int32)
        )

    def lat_copies(index, own, slot, to):
        return [
            pltpu.make_async_remote_copy(
                src_ref=given if own else held.at[slot], dst_ref=held.at[slot],
                send_sem=lat_send.at[index, part], recv_sem=lat_sem.at[slot, part],
                device_id=to, device_id_type=MESH,
            )
            for part, (given, held) in enumerate(((latent, lat_all), (rope_keys, rope_all)))
        ]

    def lat_wait(slot):
        for part, held in enumerate((lat_all, rope_all)):
            pltpu.make_async_copy(held.at[slot], held.at[slot], lat_sem.at[slot, part]).wait()

    def lat_out():
        sent = [lat_copies(k - 1, True, look + head, (seq, owner(k, core))) for k in range(1, xs)]
        return sent + [lat_copies(xs - 1, True, look + head, (seq, mate))]

    def back_out():
        return lat_copies(xs, True, shown, (seq + 1, head))

    def lat_on(k):
        return lat_copies(xs + k, False, look + owner(k, core), (seq, mate))

    def back_on(k):
        return lat_copies(2 * xs + k - 1, False, shown, (seq, owner(k, core)))

    def back_mate(i):
        return lat_copies(3 * xs - 1 + i, False, i, (seq, mate))

    def back_side(i):
        return core == (n_head - look + i) % 2

    def start(copies):
        for copy in copies:
            copy.start()

    def x_copies(k):
        return [
            pltpu.make_async_remote_copy(
                src_ref=source.at[:, pl.ds(wide * cw, cw)], dst_ref=w.at[wide + k, seq, kv],
                send_sem=x_send.at[k - 1], recv_sem=w_own.at[wide + k],
                device_id=(seq, owner(xs - k, core)), device_id_type=MESH,
            )
            for kv, source in enumerate((key_weight, value_weight))
        ]

    def own_weights(c):
        mine = w.at[c, seq]
        pltpu.make_async_copy(mine, mine, w_own.at[c]).wait()

    def ring_copies(c, t, way):
        origin = at_place(place - (t - 1)) if way == 0 else at_place(place + (t - 1))
        if t == half:
            pairs = [(w.at[c, origin, way], w.at[c, origin, way])]
        elif t == 1 and c <= wide:
            pairs = [
                (source.at[:, pl.ds(c * cw, cw)], w.at[c, origin, kv])
                for kv, source in enumerate((key_weight, value_weight))
            ]
        else:
            pairs = [(w.at[c, origin], w.at[c, origin])]
        return [
            pltpu.make_async_remote_copy(
                src_ref=src, dst_ref=dst, send_sem=w_send, recv_sem=w_recv.at[c, t - 1, way],
                device_id=(after if way == 0 else before, head), device_id_type=MESH,
            )
            for src, dst in pairs
        ]

    def ring_start(c):
        if c > wide:
            own_weights(c)
        for way in range(2):
            start(ring_copies(c, 1, way))

    def ring_take(c, t):
        for way in range(2):
            origin = at_place(place - t) if way == 0 else at_place(place + t)
            landed = w.at[c, origin, way] if t == half else w.at[c, origin]
            pltpu.make_async_copy(landed, landed, w_recv.at[c, t - 1, way]).wait()
            if t < half:
                start(ring_copies(c, t + 1, way))

    def q_copies(c):
        if c < wide:
            routes = [((head + k) % n_head,) * 2 + (head,) for k in range(1, n_head)]
        else:
            routes = [(mate, owner(c - wide, 1 - core), core)]
        return [
            pltpu.make_async_remote_copy(
                src_ref=queries.at[:, q_cols(who, min(c, wide))], dst_ref=qbuf.at[c, slot],
                send_sem=q_send.at[0 if c < wide else 1], recv_sem=q_sem.at[c],
                device_id=(seq, peer), device_id_type=MESH,
            )
            for peer, who, slot in routes
        ]

    def tile_at(c, j):
        if c >= wide:
            return 1 - core if j == 0 else core
        if j < n_head - 2:
            return (2 * x + 2 + j) % n_head
        return mate if j == n_head - 2 else head

    def o_copy(c, j):
        tile = tile_at(c, j)
        peer, who = (tile, head) if c < wide else (mate, owner(c - wide, core))
        return pltpu.make_async_remote_copy(
            src_ref=obuf.at[c, tile], dst_ref=out.at[:, o_cols(who, min(c, wide))],
            send_sem=o_send.at[0 if c < wide else 1], recv_sem=o_sem,
            device_id=(seq, peer), device_id_type=MESH,
        )

    start([copy for copies in lat_out() for copy in copies])

    @pl.when(gives)
    def _():
        start(back_out())

    ring_start(0)
    start(q_copies(0))
    ring_start(1)
    for c in range(wide, pieces):
        start(q_copies(c))

    docs = lengths.shape[0]
    first = seq * n_head * tok

    def mask_tile(j, carry):
        q_place = first + j * tok + lax.broadcasted_iota(jnp.int32, (tok, 1), 0)

        def document(d, state):
            begin, begun = state
            return begin + lengths[d], jnp.where(begin <= q_place, begin, begun)

        _, begun = lax.fori_loop(
            0, docs, document, (jnp.int32(0), jnp.zeros((tok, 1), jnp.int32)), unroll=True
        )
        k_place = first + (j - look) * tok + lax.broadcasted_iota(jnp.int32, (tok, span), 1)
        seen = (k_place >= begun) & (k_place <= q_place)
        bias[j] = jnp.where(seen, 0.0, -jnp.inf)
        return carry

    with jax.named_scope("mask"):
        lax.fori_loop(0, n_head, mask_tile, 0)

        @pl.when(seq == 0)
        def _():
            lat_all[:look] = jnp.zeros((look, tok, rank), jnp.bfloat16)
            rope_all[:look] = jnp.zeros((look, ROPE, tok), jnp.bfloat16)

        for h in range(chunk_heads):
            vbuf[:, (2 * h + 1) * VDIM:(2 * h + 2) * VDIM] = jnp.ones(
                (slots * tok, VDIM), jnp.bfloat16
            )

    def lat_relay():
        for k in range(1, xs):
            lat_wait(look + owner(k, core))
            start(lat_on(k))

    def back_relay():
        @pl.when(takes)
        def _():
            lat_wait(shown)
            for k in range(1, xs):
                start(back_on(k))

    def back_relay_mate():
        for i in range(look):
            @pl.when(back_side(i) & (seq > 0))
            def _():
                @pl.when(head != n_head - look + i)
                def _():
                    lat_wait(i)

                start(back_mate(i))

    def lat_done():
        lat_wait(look + head)
        for k in range(xs):
            lat_wait(look + owner(k, 1 - core))
        for i in range(look):
            @pl.when(jnp.logical_not(back_side(i)) & (seq > 0))
            def _():
                lat_wait(i)

    def rope_in():
        first_half = lax.broadcasted_iota(jnp.int32, (tok, 2 * ROPE), 1) < ROPE

        def fill(slot, carry):
            rope = rope_all[slot].astype(jnp.float32)
            twice = jnp.concatenate([rope, rope], axis=0).T
            at = pl.ds(pl.multiple_of(slot * tok, tok), tok)
            for h in range(chunk_heads):
                laid = jnp.where(first_half, twice, 0.0) if h % 2 == 0 else twice
                kaug[h, at, NOPE:] = laid.astype(jnp.bfloat16)
            return carry

        lax.fori_loop(0, slots, fill, 0)

    def project(c):
        if c <= wide:
            own_weights(c)
        first_slot, tiles = (0, slots) if c < wide else (2 * x, look + 2)
        parts = -(-tiles // 6)
        done = 0
        for part in range(parts):
            many = (tiles - done) // (parts - part)
            slot = first_slot + done
            done += many
            block = many * tok
            at = pl.ds(pl.multiple_of(slot * tok, tok), block)
            lat = lat_all[pl.ds(slot, many)].reshape(block, rank)
            low = lax.broadcasted_iota(jnp.int32, (block, NOPE), 1) < ROPE
            for pair in range(chunk_heads // 2):
                cols = slice(pair * 2 * NOPE, (pair + 1) * 2 * NOPE)
                k = jnp.dot(
                    lat, w[c, :, 0, :, cols].reshape(rank, 2 * NOPE),
                    preferred_element_type=jnp.float32,
                )
                kaug[2 * pair, at, :NOPE] = k[:, :NOPE].astype(jnp.bfloat16)
                turned = pltpu.roll(k[:, NOPE:], ROPE, axis=1)
                kaug[2 * pair + 1, at, :NOPE] = jnp.where(low, 0.0, turned).astype(jnp.bfloat16)
                rope_last = kaug[2 * pair + 1, at, NOPE:].astype(jnp.float32)
                kaug[2 * pair + 1, at, NOPE:] = jnp.where(low, turned, rope_last).astype(
                    jnp.bfloat16
                )
                v = jnp.dot(
                    lat, w[c, :, 1, :, cols].reshape(rank, 2 * VDIM),
                    preferred_element_type=jnp.float32,
                )
                for side in range(2):
                    begin = (2 * pair + side) * 2 * VDIM
                    vbuf[at, begin:begin + VDIM] = v[:, side * VDIM:(side + 1) * VDIM].astype(
                        jnp.bfloat16
                    )

    scale = LOG2E / math.sqrt(QK)

    def attend(c, j):
        tile = tile_at(c, j)
        place_of = tile if c < wide else 2 * x + tile
        at = pl.ds(pl.multiple_of(place_of * tok, tok), span)
        hide = bias[place_of]
        for h in range(chunk_heads):
            begin = (h // 2) * 2 * QK + (h % 2) * NOPE
            q = qbuf[c, tile, :, begin:begin + 2 * NOPE]
            s = lax.dot_general(
                q, kaug[h, at, :], (((1,), (1,)), ((), ())),
                preferred_element_type=jnp.float32,
            )
            s = s * scale + hide
            peak = jnp.max(s, axis=1, keepdims=True)
            expo = jnp.exp2(s - peak).astype(jnp.bfloat16)
            both = jnp.dot(
                expo, vbuf[at, h * 2 * VDIM:(h + 1) * 2 * VDIM],
                preferred_element_type=jnp.float32,
            )
            given = (both[:, :VDIM] / both[:, VDIM:]).astype(jnp.bfloat16)
            obuf[c, tile, :, h * VDIM:(h + 1) * VDIM] = given

    def q_in(c):
        landed = qbuf.at[c] if c < wide else qbuf.at[c, pl.ds(0, 2)]
        pltpu.make_async_copy(landed, landed, q_sem.at[c]).wait()

    def work_on(c):
        tiles = n_head if c < wide else 2

        def keys():
            with jax.named_scope(f"project{c}"):
                project(c)

        def tile(j):
            if j == 0:
                with jax.named_scope(f"q_in{c}"):
                    q_in(c)
            with jax.named_scope(f"attend{c}_{j}"):
                attend(c, j)
                if j < tiles - 1:
                    o_copy(c, j).start()
                else:
                    who = head if c < wide else owner(c - wide, core)
                    out[:, o_cols(who, min(c, wide))] = obuf[c, tile_at(c, j)]

        return [(0.8, keys)] + [(0.6, functools.partial(tile, j)) for j in range(tiles)]

    begins = {(0, half // 2): 2} | {(c - 3, half): c for c in range(3, pieces)}
    chores = {
        0: [lat_relay],
        1: [back_relay] + [lambda c=c: start(q_copies(c)) for c in range(1, min(2, wide))]
        + [lambda k=k: start(x_copies(k)) for k in range(1, xs)],
        2: [back_relay_mate],
        3: [lambda c=c: start(q_copies(c)) for c in range(2, wide)] + [lat_done, rope_in],
    }
    flight, waiting, number = [(0, 1), (1, 1)], [], 0
    while flight:
        c, t = flight.pop(0)
        with jax.named_scope(f"ring{c}_{t}"):
            ring_take(c, t)
        if t < half:
            flight.append((c, t + 1))
        if (c, t) in begins:
            ring_start(begins[c, t])
            flight.append((begins[c, t], 1))
        for chore in chores.get(number, []):
            with jax.named_scope(f"chore{number}"):
                chore()
        number += 1
        if t == half:
            waiting += work_on(c)
        room = 1.8
        while waiting and room > 0:
            cost, step = waiting.pop(0)
            step()
            room -= cost
    for _, step in waiting:
        step()

    with jax.named_scope("last"):
        landed = out.at[:, pl.ds(0, (wide * (n_head - 1) + xs) * cw)]
        pltpu.make_async_copy(landed, landed, o_sem).wait()

    def sent(ref, sem):
        pltpu.make_async_copy(ref, ref, sem).wait()

    with jax.named_scope("sends"):
        sent(obuf.at[pl.ds(0, wide), pl.ds(0, n_head - 1)], o_send.at[0])
        sent(obuf.at[pl.ds(wide, xs), pl.ds(0, 1)], o_send.at[1])
        sent(qbuf.at[pl.ds(0, wide), pl.ds(0, n_head - 1)], q_send.at[0])
        sent(qbuf.at[pl.ds(wide, xs), pl.ds(0, 1)], q_send.at[1])
        sent(w.at[:, pl.ds(0, n_seq - 1)], w_send)
        for k in range(1, xs):
            sent(w.at[wide + k, seq], x_send.at[k - 1])
        for copies in lat_out() + [lat_on(k) for k in range(1, xs)]:
            for copy in copies:
                copy.wait_send()

        @pl.when(gives)
        def _():
            for copy in back_out():
                copy.wait_send()

        @pl.when(takes)
        def _():
            for k in range(1, xs):
                for copy in back_on(k):
                    copy.wait_send()

        for i in range(look):
            @pl.when(back_side(i) & (seq > 0))
            def _():
                for copy in back_mate(i):
                    copy.wait_send()


def shards(queries, latent, rope_keys, key_weight, value_weight, doc_lengths):
    n_seq, n_head = lax.axis_size("seq"), lax.axis_size("head")
    tok, rank = latent.shape
    rows = key_weight.shape[0]
    local_heads = key_weight.shape[1] // NOPE
    docs = doc_lengths.shape[0]
    slot_rows = n_seq * n_head * tok // docs
    look = 2 * -(-slot_rows // tok) - 1
    chunk_heads = min(4, local_heads)
    wide = local_heads // chunk_heads - 1
    xs = n_head // 2
    pieces = wide + xs
    slots, span, half = look + n_head, (look + 1) * tok, n_seq // 2
    cw, qw = chunk_heads * NOPE, chunk_heads * QK
    anywhere = pl.BlockSpec(memory_space=pl.ANY)
    dma = pltpu.SemaphoreType.DMA
    bf16 = jnp.bfloat16
    return pl.pallas_call(
        functools.partial(kernel, (n_seq, n_head, look, wide, chunk_heads)),
        out_shape=pltpu.VMEM((tok, n_head * local_heads * VDIM), bf16),
        in_specs=[anywhere] * 5 + [pl.BlockSpec(memory_space=pltpu.SMEM)],
        out_specs=pl.BlockSpec(memory_space=pltpu.VMEM),
        scratch_shapes=[
            pltpu.VMEM((slots, tok, rank), bf16),
            pltpu.VMEM((slots, ROPE, tok), bf16),
            pltpu.VMEM((pieces, n_seq, 2, rows, cw), bf16),
            pltpu.VMEM((pieces, n_head, tok, qw), bf16),
            pltpu.VMEM((chunk_heads, slots * tok, 2 * NOPE), bf16),
            pltpu.VMEM((slots * tok, 2 * cw), bf16),
            pltpu.VMEM((n_head, tok, span), jnp.float32),
            pltpu.VMEM((pieces, n_head, tok, cw), bf16),
            dma((slots, 2)),
            dma((3 * xs - 1 + look, 2)),
            dma((pieces,)),
            dma((pieces, half, 2)),
            dma,
            dma((xs - 1,)),
            dma((pieces,)),
            dma((2,)),
            dma,
            dma((2,)),
        ],
        compiler_params=pltpu.CompilerParams(collective_id=0, has_side_effects=True),
    )(queries, latent, rope_keys.T, key_weight, value_weight, doc_lengths)


def solution(mesh):
    placed = (
        P(("seq", "head"), None),
        P(("seq", "head"), None),
        P(("seq", "head"), None),
        P("seq", "head"),
        P("seq", "head"),
        P(),
    )
    return jax.shard_map(
        shards, mesh=mesh, in_specs=placed, out_specs=P(("seq", "head"), None), check_vma=False
    )
```

time: 78 us -> 63.5 us (0.81)
  Pallas kernels: 72.8 us -> 61.6 us
  local copies, waits for them, and re-layouts: 4.53 us -> 1.32 us
    pallas_call x1, Pallas kernels: 72.8 us -> 61.6 us  [shards(): pl.pallas_call(functools.partial(kernel, (n_seq, n_head, look, wide, chun...]
    unnamed x2 -> x1, local copies, waits for them, and re-layouts: 4.53 us -> 1.32 us
where the time goes in v1:
time: 63.5 us; the launch traced here: 62.9 us
  Pallas kernels  61.6 us (97%)
  local copies, waits for them, and re-layouts  1.32 us (2%)
    pallas_call x1, Pallas kernels, shards(): pl.pallas_call(functools.partial(kernel, (n_seq, n_head, look, wide, chun...  61.6 us
    unnamed x1, local copies, waits for them, and re-layouts  1.32 us

profile of v1, /device:TPU:1, one launch (start us, length us, event | category | flops | bytes accessed | tf_op | source)
XLA Modules:
  0.0 62.9 jit_solution(17210861438357032131)
XLA Ops:
  0.0 61.6 %shard_map.64 = bf16[128,8192]{1,0:T(8,128)(2,1)S(1)} custom-call(bf16[128,12288]{1,0:T(8,128)(2,1)} %queries.1, bf16[128,512]{1,0:T(8,128)(2,1)} %latent.1, bf16[64,128]{1,0:T(8,128)(2,1)} %bitcast.1, bf16[64,2048]{1,0:T(8,128)(2,1)} %key_weight.1, bf16[64,2048]{1,0:T(8,128)(2,1)} %value_weight.1, s32[32]{0:T(128)} %lengths.1), custom_call_target="tpu_custom_call" | custom-call | tf_op jit(solution)/shard_map/pallas_call | solution.py:479
  61.6 1.3 %copy.8 = bf16[128,8192]{1,0:T(8,128)(2,1)} copy(bf16[128,8192]{1,0:T(8,128)(2,1)S(1)} %shard_map.64) | data formatting | bytes 4194304

commit v2 on v1

--- a/solution.py
+++ b/solution.py
@@ -17,10 +17,30 @@
 MESH = pl.DeviceIdType.MESH
 
 
+def ring_order(pieces, wide, steps_of):
+    if (pieces, wide, steps_of(0)) == (5, 3, 4):
+        steps = (1, 11, 2, 12, 3, 31, 21, 13, 4, 22, 14, 32, 41, 23, 42, 24, 33, 43, 34)
+        return [divmod(step, 10) for step in steps], {4: (2, 2)}
+    first = [0, wide] + list(range(1, wide))
+    flight, later, order = [(c, 1) for c in first[:2]], first[2:] + list(range(wide + 1, pieces)), []
+    while flight:
+        c, t = flight.pop(0)
+        order.append((c, t))
+        if t < steps_of(c):
+            flight.append((c, t + 1))
+        if t >= steps_of(c) // 2 and later and len(flight) < 3:
+            flight.append((later.pop(0), 1))
+    holds = {}
+    for c in range(wide + 1, pieces):
+        at = order.index((c, 1))
+        holds[c] = order[max(at - 2, order.index((wide, 1)))]
+    return order, holds
+
+
 def kernel(
-    sizes, queries, latent, rope_keys, key_weight, value_weight, lengths, out,
-    lat_all, rope_all, w, qbuf, kaug, vbuf, bias, obuf,
-    lat_sem, lat_send, w_own, w_recv, w_send, x_send, q_sem, q_send, o_sem, o_send,
+    sizes, queries, latent, rope_keys, key_weight, value_weight, lengths_in, out,
+    lat_all, rope_all, w, qbuf, kaug, vbuf, bias, obuf, lengths,
+    len_sem, lat_sem, lat_send, w_own, w_recv, w_send, x_send, x_recv, q_sem, q_send, o_sem, o_send,
 ):
     n_seq, n_head, look, wide, chunk_heads = sizes
     tok, rank = latent.shape
@@ -78,14 +98,14 @@
         return pl.ds(pl.multiple_of(who * o_all + c * cw, 128), cw)
 
     def own_copies():
-        mine = look + head
-        pltpu.make_async_copy(latent, lat_all.at[mine], lat_sem.at[mine, 0]).start()
-        pltpu.make_async_copy(rope_keys, rope_all.at[mine], lat_sem.at[mine, 1]).start()
         for c in range(wide + 1):
             for kv, source in enumerate((key_weight, value_weight)):
                 pltpu.make_async_copy(
                     source.at[:, pl.ds(c * cw, cw)], w.at[c, seq, kv], w_own.at[c]
                 ).start()
+        mine = look + head
+        pltpu.make_async_copy(latent, lat_all.at[mine], lat_sem.at[mine, 0]).start()
+        pltpu.make_async_copy(rope_keys, rope_all.at[mine], lat_sem.at[mine, 1]).start()
         for c in range(wide):
             pltpu.make_async_copy(
                 queries.at[:, q_cols(head, c)], qbuf.at[c, head], q_sem.at[c]
@@ -97,40 +117,44 @@
             ).start()
 
     own_copies()
+    pltpu.make_async_copy(lengths_in, lengths, len_sem).start()
     with jax.named_scope("barrier"):
         pl.semaphore_wait(
             barrier, n_head + 1 + gives.astype(jnp.int32) + takes.astype(jnp.int32)
         )
 
-    def lat_copies(index, own, slot, to):
+    def lat_copies(index, slot, to, landing):
         return [
             pltpu.make_async_remote_copy(
-                src_ref=given if own else held.at[slot], dst_ref=held.at[slot],
-                send_sem=lat_send.at[index, part], recv_sem=lat_sem.at[slot, part],
+                src_ref=held.at[slot], dst_ref=held.at[landing],
+                send_sem=lat_send.at[index, part], recv_sem=lat_sem.at[landing, part],
                 device_id=to, device_id_type=MESH,
             )
-            for part, (given, held) in enumerate(((latent, lat_all), (rope_keys, rope_all)))
+            for part, held in enumerate((lat_all, rope_all))
         ]
 
     def lat_wait(slot):
         for part, held in enumerate((lat_all, rope_all)):
             pltpu.make_async_copy(held.at[slot], held.at[slot], lat_sem.at[slot, part]).wait()
 
+    mine = look + head
+
     def lat_out():
-        sent = [lat_copies(k - 1, True, look + head, (seq, owner(k, core))) for k in range(1, xs)]
-        return sent + [lat_copies(xs - 1, True, look + head, (seq, mate))]
+        sent = [lat_copies(k - 1, mine, (seq, owner(k, core)), mine) for k in range(1, xs)]
+        return sent + [lat_copies(xs - 1, mine, (seq, mate), mine)]
 
     def back_out():
-        return lat_copies(xs, True, shown, (seq + 1, head))
+        return lat_copies(xs, mine, (seq + 1, head), shown)
 
     def lat_on(k):
-        return lat_copies(xs + k, False, look + owner(k, core), (seq, mate))
+        slot = look + owner(k, core)
+        return lat_copies(xs + k, slot, (seq, mate), slot)
 
     def back_on(k):
-        return lat_copies(2 * xs + k - 1, False, shown, (seq, owner(k, core)))
+        return lat_copies(2 * xs + k - 1, shown, (seq, owner(k, core)), shown)
 
     def back_mate(i):
-        return lat_copies(3 * xs - 1 + i, False, i, (seq, mate))
+        return lat_copies(3 * xs - 1 + i, i, (seq, mate), i)
 
     def back_side(i):
         return core == (n_head - look + i) % 2
@@ -139,52 +163,46 @@
         for copy in copies:
             copy.start()
 
-    def x_copies(k):
-        return [
-            pltpu.make_async_remote_copy(
-                src_ref=source.at[:, pl.ds(wide * cw, cw)], dst_ref=w.at[wide + k, seq, kv],
-                send_sem=x_send.at[k - 1], recv_sem=w_own.at[wide + k],
-                device_id=(seq, owner(xs - k, core)), device_id_type=MESH,
-            )
-            for kv, source in enumerate((key_weight, value_weight))
-        ]
-
-    def own_weights(c):
-        mine = w.at[c, seq]
-        pltpu.make_async_copy(mine, mine, w_own.at[c]).wait()
-
-    def ring_copies(c, t, way):
-        origin = at_place(place - (t - 1)) if way == 0 else at_place(place + (t - 1))
-        if t == half:
-            pairs = [(w.at[c, origin, way], w.at[c, origin, way])]
-        elif t == 1 and c <= wide:
-            pairs = [
-                (source.at[:, pl.ds(c * cw, cw)], w.at[c, origin, kv])
-                for kv, source in enumerate((key_weight, value_weight))
-            ]
+    def x_copy(k, near):
+        rows_of = seq if near == 0 else before
+        return pltpu.make_async_remote_copy(
+            src_ref=w.at[wide, rows_of], dst_ref=w.at[wide + k, rows_of],
+            send_sem=x_send.at[k - 1, near], recv_sem=x_recv.at[k - 1, near],
+            device_id=(seq, owner(xs - k, core)), device_id_type=MESH,
+        )
+
+    def landed_rows(c):
+        if c <= wide:
+            pltpu.make_async_copy(w.at[c, seq], w.at[c, seq], w_own.at[c]).wait()
         else:
-            pairs = [(w.at[c, origin], w.at[c, origin])]
-        return [
-            pltpu.make_async_remote_copy(
-                src_ref=src, dst_ref=dst, send_sem=w_send, recv_sem=w_recv.at[c, t - 1, way],
-                device_id=(after if way == 0 else before, head), device_id_type=MESH,
-            )
-            for src, dst in pairs
-        ]
-
-    def ring_start(c):
-        if c > wide:
-            own_weights(c)
+            for near, rows_of in enumerate((seq, before)):
+                here = w.at[c, rows_of]
+                pltpu.make_async_copy(here, here, x_recv.at[c - wide - 1, near]).wait()
+
+    def steps_of(c):
+        return half if c <= wide else half - 1
+
+    def origin_at(c, t, way):
+        return at_place(place - t - (c > wide)) if way == 0 else at_place(place + t)
+
+    def ring_copy(c, t, way):
+        origin = origin_at(c, t - 1, way)
+        block = w.at[c, origin, way] if t == half else w.at[c, origin]
+        return pltpu.make_async_remote_copy(
+            src_ref=block, dst_ref=block, send_sem=w_send.at[0 if c <= wide else 1],
+            recv_sem=w_recv.at[c, t - 1],
+            device_id=(after if way == 0 else before, head), device_id_type=MESH,
+        )
+
+    def ring_send(c, t):
+        if t == 1 and c > wide:
+            landed_rows(c)
         for way in range(2):
-            start(ring_copies(c, 1, way))
+            ring_copy(c, t, way).start()
 
     def ring_take(c, t):
-        for way in range(2):
-            origin = at_place(place - t) if way == 0 else at_place(place + t)
-            landed = w.at[c, origin, way] if t == half else w.at[c, origin]
-            pltpu.make_async_copy(landed, landed, w_recv.at[c, t - 1, way]).wait()
-            if t < half:
-                start(ring_copies(c, t + 1, way))
+        landed = w.at[c, 0] if t == half else w.at[c, pl.ds(0, 2)]
+        pltpu.make_async_copy(landed, landed, w_recv.at[c, t - 1]).wait()
 
     def q_copies(c):
         if c < wide:
@@ -216,15 +234,20 @@
             device_id=(seq, peer), device_id_type=MESH,
         )
 
+    order, holds = ring_order(pieces, wide, steps_of)
+    for c in range(wide + 1):
+        landed_rows(c)
+        if c == 0:
+            ring_send(*order[0])
+    ring_send(*order[1])
+    lat_wait(mine)
     start([copy for copies in lat_out() for copy in copies])
+    start(q_copies(0))
 
     @pl.when(gives)
     def _():
         start(back_out())
 
-    ring_start(0)
-    start(q_copies(0))
-    ring_start(1)
     for c in range(wide, pieces):
         start(q_copies(c))
 
@@ -247,6 +270,7 @@
         return carry
 
     with jax.named_scope("mask"):
+        pltpu.make_async_copy(lengths_in, lengths, len_sem).wait()
         lax.fori_loop(0, n_head, mask_tile, 0)
 
         @pl.when(seq == 0)
@@ -282,7 +306,6 @@
                 start(back_mate(i))
 
     def lat_done():
-        lat_wait(look + head)
         for k in range(xs):
             lat_wait(look + owner(k, 1 - core))
         for i in range(look):
@@ -305,8 +328,6 @@
         lax.fori_loop(0, slots, fill, 0)
 
     def project(c):
-        if c <= wide:
-            own_weights(c)
         first_slot, tiles = (0, slots) if c < wide else (2 * x, look + 2)
         parts = -(-tiles // 6)
         done = 0
@@ -343,28 +364,45 @@
 
     scale = LOG2E / math.sqrt(QK)
 
-    def attend(c, j):
-        tile = tile_at(c, j)
-        place_of = tile if c < wide else 2 * x + tile
-        at = pl.ds(pl.multiple_of(place_of * tok, tok), span)
-        hide = bias[place_of]
-        for h in range(chunk_heads):
+    def attend(c, tiles, then):
+        def places(tile):
+            place_of = tile if c < wide else 2 * x + tile
+            return place_of, pl.ds(pl.multiple_of(place_of * tok, tok), span)
+
+        def scores(tile, h):
             begin = (h // 2) * 2 * QK + (h % 2) * NOPE
-            q = qbuf[c, tile, :, begin:begin + 2 * NOPE]
-            s = lax.dot_general(
-                q, kaug[h, at, :], (((1,), (1,)), ((), ())),
-                preferred_element_type=jnp.float32,
+            return lax.dot_general(
+                qbuf[c, tile, :, begin:begin + 2 * NOPE], kaug[h, places(tile)[1], :],
+                (((1,), (1,)), ((), ())), preferred_element_type=jnp.float32,
             )
-            s = s * scale + hide
+
+        def weights(tile, s):
+            s = s * scale + bias[places(tile)[0]]
             peak = jnp.max(s, axis=1, keepdims=True)
-            expo = jnp.exp2(s - peak).astype(jnp.bfloat16)
+            return jnp.exp2(s - peak).astype(jnp.bfloat16)
+
+        def mix(tile, h, expo):
             both = jnp.dot(
-                expo, vbuf[at, h * 2 * VDIM:(h + 1) * 2 * VDIM],
+                expo, vbuf[places(tile)[1], h * 2 * VDIM:(h + 1) * 2 * VDIM],
                 preferred_element_type=jnp.float32,
             )
             given = (both[:, :VDIM] / both[:, VDIM:]).astype(jnp.bfloat16)
             obuf[c, tile, :, h * VDIM:(h + 1) * VDIM] = given
 
+        items = [(tile, h) for tile in tiles for h in range(chunk_heads)]
+        held = [scores(tile, h) for tile, h in items]
+        expo = {}
+        for i, (tile, h) in enumerate(items):
+            expo[i] = weights(tile, held[i])
+            if i > 0:
+                mix(*items[i - 1], expo.pop(i - 1))
+            if i == chunk_heads and c >= wide:
+                then[0]()
+        mix(*items[-1], expo.pop(len(items) - 1))
+        if c < wide:
+            then[0]()
+        then[1]()
+
     def q_in(c):
         landed = qbuf.at[c] if c < wide else qbuf.at[c, pl.ds(0, 2)]
         pltpu.make_async_copy(landed, landed, q_sem.at[c]).wait()
@@ -373,46 +411,49 @@
         tiles = n_head if c < wide else 2
 
         def keys():
+            with jax.named_scope(f"q_in{c}"):
+                q_in(c)
             with jax.named_scope(f"project{c}"):
                 project(c)
 
-        def tile(j):
-            if j == 0:
-                with jax.named_scope(f"q_in{c}"):
-                    q_in(c)
+        def pair(j):
+            def keep():
+                who = head if c < wide else owner(c - wide, core)
+                out[:, o_cols(who, min(c, wide))] = obuf[c, tile_at(c, j + 1)]
+
+            first_sent = o_copy(c, j).start
+            second_sent = o_copy(c, j + 1).start if j + 2 < tiles else keep
             with jax.named_scope(f"attend{c}_{j}"):
-                attend(c, j)
-                if j < tiles - 1:
-                    o_copy(c, j).start()
-                else:
-                    who = head if c < wide else owner(c - wide, core)
-                    out[:, o_cols(who, min(c, wide))] = obuf[c, tile_at(c, j)]
-
-        return [(0.8, keys)] + [(0.6, functools.partial(tile, j)) for j in range(tiles)]
-
-    begins = {(0, half // 2): 2} | {(c - 3, half): c for c in range(3, pieces)}
+                attend(c, [tile_at(c, j), tile_at(c, j + 1)], (first_sent, second_sent))
+
+        return [(0.8, keys)] + [(0.8, functools.partial(pair, j)) for j in range(0, tiles, 2)]
+
     chores = {
-        0: [lat_relay],
-        1: [back_relay] + [lambda c=c: start(q_copies(c)) for c in range(1, min(2, wide))]
-        + [lambda k=k: start(x_copies(k)) for k in range(1, xs)],
-        2: [back_relay_mate],
-        3: [lambda c=c: start(q_copies(c)) for c in range(2, wide)] + [lat_done, rope_in],
+        (0, 1): [lat_relay],
+        (1, 1): [back_relay] + [lambda c=c: start(q_copies(c)) for c in range(1, min(2, wide))]
+        + [lambda k=k: x_copy(k, 0).start() for k in range(1, xs)],
+        (0, 2): [back_relay_mate],
+        (1, 2): [lat_done, rope_in],
     }
-    flight, waiting, number = [(0, 1), (1, 1)], [], 0
-    while flight:
-        c, t = flight.pop(0)
+    chores.setdefault((wide, 1), []).extend(
+        [lambda k=k: x_copy(k, 1).start() for k in range(1, xs)]
+        + [lambda c=c: start(q_copies(c)) for c in range(2, wide)]
+    )
+    unsent, waiting, taken = order[2:], [], set()
+    for c, t in order:
         with jax.named_scope(f"ring{c}_{t}"):
             ring_take(c, t)
-        if t < half:
-            flight.append((c, t + 1))
-        if (c, t) in begins:
-            ring_start(begins[c, t])
-            flight.append((begins[c, t], 1))
-        for chore in chores.get(number, []):
-            with jax.named_scope(f"chore{number}"):
+        taken.add((c, t))
+        while unsent:
+            ahead, step = unsent[0]
+            need = (ahead, step - 1) if step > 1 else holds.get(ahead)
+            if need is not None and need not in taken:
+                break
+            ring_send(*unsent.pop(0))
+        for chore in chores.get((c, t), []):
+            with jax.named_scope("chore"):
                 chore()
-        number += 1
-        if t == half:
+        if t == steps_of(c):
             waiting += work_on(c)
         room = 1.8
         while waiting and room > 0:
@@ -434,9 +475,11 @@
         sent(obuf.at[pl.ds(wide, xs), pl.ds(0, 1)], o_send.at[1])
         sent(qbuf.at[pl.ds(0, wide), pl.ds(0, n_head - 1)], q_send.at[0])
         sent(qbuf.at[pl.ds(wide, xs), pl.ds(0, 1)], q_send.at[1])
-        sent(w.at[:, pl.ds(0, n_seq - 1)], w_send)
+        sent(w.at[pl.ds(0, wide + 1), pl.ds(0, n_seq - 1)], w_send.at[0])
+        sent(w.at[pl.ds(wide + 1, xs - 1), pl.ds(0, n_seq - 2)], w_send.at[1])
         for k in range(1, xs):
-            sent(w.at[wide + k, seq], x_send.at[k - 1])
+            for near in range(2):
+                x_copy(k, near).wait_send()
         for copies in lat_out() + [lat_on(k) for k in range(1, xs)]:
             for copy in copies:
                 copy.wait_send()
@@ -479,7 +522,7 @@
     return pl.pallas_call(
         functools.partial(kernel, (n_seq, n_head, look, wide, chunk_heads)),
         out_shape=pltpu.VMEM((tok, n_head * local_heads * VDIM), bf16),
-        in_specs=[anywhere] * 5 + [pl.BlockSpec(memory_space=pltpu.SMEM)],
+        in_specs=[anywhere] * 6,
         out_specs=pl.BlockSpec(memory_space=pltpu.VMEM),
         scratch_shapes=[
             pltpu.VMEM((slots, tok, rank), bf16),
@@ -490,12 +533,15 @@
             pltpu.VMEM((slots * tok, 2 * cw), bf16),
             pltpu.VMEM((n_head, tok, span), jnp.float32),
             pltpu.VMEM((pieces, n_head, tok, cw), bf16),
+            pltpu.SMEM((docs,), jnp.int32),
+            dma,
             dma((slots, 2)),
             dma((3 * xs - 1 + look, 2)),
-            dma((pieces,)),
-            dma((pieces, half, 2)),
-            dma,
-            dma((xs - 1,)),
+            dma((wide + 1,)),
+            dma((pieces, half)),
+            dma((2,)),
+            dma((xs - 1, 2)),
+            dma((xs - 1, 2)),
             dma((pieces,)),
             dma((2,)),
             dma,

time: 63.5 us -> 58.4 us (0.920)
  Pallas kernels: 61.6 us -> 56.8 us
    pallas_call x1, Pallas kernels: 61.6 us -> 56.8 us  [shards(): pl.pallas_call(functools.partial(kernel, (n_seq, n_head, look, wide, chun...]
where the time goes in v2:
time: 58.4 us; the launch traced here: 58.1 us
  Pallas kernels  56.8 us (97%)
  local copies, waits for them, and re-layouts  1.32 us (2%)
    pallas_call x1, Pallas kernels, shards(): pl.pallas_call(functools.partial(kernel, (n_seq, n_head, look, wide, chun...  56.8 us
    unnamed x1, local copies, waits for them, and re-layouts  1.32 us

profile of v2, /device:TPU:1, one launch (start us, length us, event | category | flops | bytes accessed | tf_op | source)
XLA Modules:
  0.0 58.1 jit_solution(16971786453042656642)
XLA Ops:
  0.0 56.8 %shard_map.64 = bf16[128,8192]{1,0:T(8,128)(2,1)S(1)} custom-call(bf16[128,12288]{1,0:T(8,128)(2,1)} %queries.1, bf16[128,512]{1,0:T(8,128)(2,1)} %latent.1, bf16[64,128]{1,0:T(8,128)(2,1)} %bitcast.1, bf16[64,2048]{1,0:T(8,128)(2,1)} %key_weight.1, bf16[64,2048]{1,0:T(8,128)(2,1)} %value_weight.1, s32[32]{0:T(128)} %lengths_in.1), custom_call_target="tpu_custom_call" | custom-call | tf_op jit(solution)/shard_map/pallas_call | solution.py:522
  56.8 1.3 %copy.8 = bf16[128,8192]{1,0:T(8,128)(2,1)} copy(bf16[128,8192]{1,0:T(8,128)(2,1)S(1)} %shard_map.64) | data formatting | bytes 4194304

commit v3 on v2

--- a/solution.py
+++ b/solution.py
@@ -94,14 +94,11 @@
     def q_cols(who, c):
         return pl.ds(pl.multiple_of(who * q_all + c * qw, 128), qw)
 
-    def o_cols(who, c):
-        return pl.ds(pl.multiple_of(who * o_all + c * cw, 128), cw)
-
     def own_copies():
         for c in range(wide + 1):
             for kv, source in enumerate((key_weight, value_weight)):
                 pltpu.make_async_copy(
-                    source.at[:, pl.ds(c * cw, cw)], w.at[c, seq, kv], w_own.at[c]
+                    source.at[:, pl.ds(c * cw, cw)], w.at[c, seq, kv], w_own
                 ).start()
         mine = look + head
         pltpu.make_async_copy(latent, lat_all.at[mine], lat_sem.at[mine, 0]).start()
@@ -167,23 +164,20 @@
         rows_of = seq if near == 0 else before
         return pltpu.make_async_remote_copy(
             src_ref=w.at[wide, rows_of], dst_ref=w.at[wide + k, rows_of],
-            send_sem=x_send.at[k - 1, near], recv_sem=x_recv.at[k - 1, near],
+            send_sem=x_send.at[k - 1], recv_sem=x_recv.at[k - 1],
             device_id=(seq, owner(xs - k, core)), device_id_type=MESH,
         )
 
-    def landed_rows(c):
-        if c <= wide:
-            pltpu.make_async_copy(w.at[c, seq], w.at[c, seq], w_own.at[c]).wait()
-        else:
-            for near, rows_of in enumerate((seq, before)):
-                here = w.at[c, rows_of]
-                pltpu.make_async_copy(here, here, x_recv.at[c - wide - 1, near]).wait()
+    def arrive(ref, sem):
+        pltpu.make_async_copy(ref, ref, sem).wait()
 
     def steps_of(c):
         return half if c <= wide else half - 1
 
     def origin_at(c, t, way):
         return at_place(place - t - (c > wide)) if way == 0 else at_place(place + t)
+
+    pairs = chunk_heads // 2
 
     def ring_copy(c, t, way):
         origin = origin_at(c, t - 1, way)
@@ -196,13 +190,14 @@
 
     def ring_send(c, t):
         if t == 1 and c > wide:
-            landed_rows(c)
+            arrive(w.at[c, pl.ds(0, 2)], x_recv.at[c - wide - 1])
         for way in range(2):
             ring_copy(c, t, way).start()
 
     def ring_take(c, t):
-        landed = w.at[c, 0] if t == half else w.at[c, pl.ds(0, 2)]
-        pltpu.make_async_copy(landed, landed, w_recv.at[c, t - 1]).wait()
+        arrive(w.at[c, 0] if t == half else w.at[c, pl.ds(0, 2)], w_recv.at[c, t - 1])
+
+    pairs = chunk_heads // 2
 
     def q_copies(c):
         if c < wide:
@@ -225,20 +220,21 @@
             return (2 * x + 2 + j) % n_head
         return mate if j == n_head - 2 else head
 
+    def o_cols(who, c):
+        return pl.ds(pl.multiple_of(who * o_all + min(c, wide) * cw, 128), cw)
+
     def o_copy(c, j):
         tile = tile_at(c, j)
         peer, who = (tile, head) if c < wide else (mate, owner(c - wide, core))
         return pltpu.make_async_remote_copy(
-            src_ref=obuf.at[c, tile], dst_ref=out.at[:, o_cols(who, min(c, wide))],
+            src_ref=obuf.at[c, tile], dst_ref=out.at[:, o_cols(who, c)],
             send_sem=o_send.at[0 if c < wide else 1], recv_sem=o_sem,
             device_id=(seq, peer), device_id_type=MESH,
         )
 
     order, holds = ring_order(pieces, wide, steps_of)
-    for c in range(wide + 1):
-        landed_rows(c)
-        if c == 0:
-            ring_send(*order[0])
+    arrive(w.at[pl.ds(0, wide + 1), 0], w_own)
+    ring_send(*order[0])
     ring_send(*order[1])
     lat_wait(mine)
     start([copy for copies in lat_out() for copy in copies])
@@ -339,12 +335,16 @@
             at = pl.ds(pl.multiple_of(slot * tok, tok), block)
             lat = lat_all[pl.ds(slot, many)].reshape(block, rank)
             low = lax.broadcasted_iota(jnp.int32, (block, NOPE), 1) < ROPE
-            for pair in range(chunk_heads // 2):
+
+            def up(kv, pair):
                 cols = slice(pair * 2 * NOPE, (pair + 1) * 2 * NOPE)
-                k = jnp.dot(
-                    lat, w[c, :, 0, :, cols].reshape(rank, 2 * NOPE),
+                return jnp.dot(
+                    lat, w[c, :, kv, :, cols].reshape(rank, 2 * NOPE),
                     preferred_element_type=jnp.float32,
                 )
+
+            for pair in range(pairs):
+                k = up(0, pair)
                 kaug[2 * pair, at, :NOPE] = k[:, :NOPE].astype(jnp.bfloat16)
                 turned = pltpu.roll(k[:, NOPE:], ROPE, axis=1)
                 kaug[2 * pair + 1, at, :NOPE] = jnp.where(low, 0.0, turned).astype(jnp.bfloat16)
@@ -352,10 +352,8 @@
                 kaug[2 * pair + 1, at, NOPE:] = jnp.where(low, turned, rope_last).astype(
                     jnp.bfloat16
                 )
-                v = jnp.dot(
-                    lat, w[c, :, 1, :, cols].reshape(rank, 2 * VDIM),
-                    preferred_element_type=jnp.float32,
-                )
+            for pair in range(pairs):
+                v = up(1, pair)
                 for side in range(2):
                     begin = (2 * pair + side) * 2 * VDIM
                     vbuf[at, begin:begin + VDIM] = v[:, side * VDIM:(side + 1) * VDIM].astype(
@@ -396,10 +394,10 @@
             expo[i] = weights(tile, held[i])
             if i > 0:
                 mix(*items[i - 1], expo.pop(i - 1))
-            if i == chunk_heads and c >= wide:
+            if i == chunk_heads and c == last:
                 then[0]()
         mix(*items[-1], expo.pop(len(items) - 1))
-        if c < wide:
+        if c != last:
             then[0]()
         then[1]()
 
@@ -407,26 +405,26 @@
         landed = qbuf.at[c] if c < wide else qbuf.at[c, pl.ds(0, 2)]
         pltpu.make_async_copy(landed, landed, q_sem.at[c]).wait()
 
+    last = order[-1][0]
+
     def work_on(c):
         tiles = n_head if c < wide else 2
-
-        def keys():
-            with jax.named_scope(f"q_in{c}"):
-                q_in(c)
-            with jax.named_scope(f"project{c}"):
-                project(c)
 
         def pair(j):
             def keep():
                 who = head if c < wide else owner(c - wide, core)
-                out[:, o_cols(who, min(c, wide))] = obuf[c, tile_at(c, j + 1)]
-
-            first_sent = o_copy(c, j).start
+                out[:, o_cols(who, c)] = obuf[c, tile_at(c, j + 1)]
+
             second_sent = o_copy(c, j + 1).start if j + 2 < tiles else keep
-            with jax.named_scope(f"attend{c}_{j}"):
-                attend(c, [tile_at(c, j), tile_at(c, j + 1)], (first_sent, second_sent))
-
-        return [(0.8, keys)] + [(0.8, functools.partial(pair, j)) for j in range(0, tiles, 2)]
+            if j == 0:
+                with jax.named_scope(f"q_in{c}"):
+                    q_in(c)
+            with jax.named_scope(f"work{c}_{j}"):
+                if j == 0:
+                    project(c)
+                attend(c, [tile_at(c, j), tile_at(c, j + 1)], (o_copy(c, j).start, second_sent))
+
+        return [(0.8, functools.partial(pair, j)) for j in range(0, tiles, 2)]
 
     chores = {
         (0, 1): [lat_relay],
@@ -467,19 +465,15 @@
         landed = out.at[:, pl.ds(0, (wide * (n_head - 1) + xs) * cw)]
         pltpu.make_async_copy(landed, landed, o_sem).wait()
 
-    def sent(ref, sem):
-        pltpu.make_async_copy(ref, ref, sem).wait()
-
     with jax.named_scope("sends"):
-        sent(obuf.at[pl.ds(0, wide), pl.ds(0, n_head - 1)], o_send.at[0])
-        sent(obuf.at[pl.ds(wide, xs), pl.ds(0, 1)], o_send.at[1])
-        sent(qbuf.at[pl.ds(0, wide), pl.ds(0, n_head - 1)], q_send.at[0])
-        sent(qbuf.at[pl.ds(wide, xs), pl.ds(0, 1)], q_send.at[1])
-        sent(w.at[pl.ds(0, wide + 1), pl.ds(0, n_seq - 1)], w_send.at[0])
-        sent(w.at[pl.ds(wide + 1, xs - 1), pl.ds(0, n_seq - 2)], w_send.at[1])
+        arrive(obuf.at[pl.ds(0, wide), pl.ds(0, n_head - 1)], o_send.at[0])
+        arrive(obuf.at[pl.ds(wide, xs), pl.ds(0, 1)], o_send.at[1])
+        arrive(qbuf.at[pl.ds(0, wide), pl.ds(0, n_head - 1)], q_send.at[0])
+        arrive(qbuf.at[pl.ds(wide, xs), pl.ds(0, 1)], q_send.at[1])
+        arrive(w.at[pl.ds(0, wide + 1), pl.ds(0, n_seq - 1)], w_send.at[0])
+        arrive(w.at[pl.ds(wide + 1, xs - 1), pl.ds(0, n_seq - 2)], w_send.at[1])
         for k in range(1, xs):
-            for near in range(2):
-                x_copy(k, near).wait_send()
+            arrive(w.at[wide, pl.ds(0, 2)], x_send.at[k - 1])
         for copies in lat_out() + [lat_on(k) for k in range(1, xs)]:
             for copy in copies:
                 copy.wait_send()
@@ -537,11 +531,11 @@
             dma,
             dma((slots, 2)),
             dma((3 * xs - 1 + look, 2)),
-            dma((wide + 1,)),
+            dma,
             dma((pieces, half)),
             dma((2,)),
-            dma((xs - 1, 2)),
-            dma((xs - 1, 2)),
+            dma((xs - 1,)),
+            dma((xs - 1,)),
             dma((pieces,)),
             dma((2,)),
             dma,

time: 58.4 us -> 58.2 us (level)
  no operation moved by 1% of the time
where the time goes in v3:
time: 58.2 us; the launch traced here: 57.7 us
  Pallas kernels  56.4 us (97%)
  local copies, waits for them, and re-layouts  1.32 us (2%)
    pallas_call x1, Pallas kernels, shards(): pl.pallas_call(functools.partial(kernel, (n_seq, n_head, look, wide, chun...  56.4 us
    unnamed x1, local copies, waits for them, and re-layouts  1.32 us

profile of v3, /device:TPU:1, one launch (start us, length us, event | category | flops | bytes accessed | tf_op | source)
XLA Modules:
  0.0 57.7 jit_solution(3034191952245439563)
XLA Ops:
  0.0 56.4 %shard_map.64 = bf16[128,8192]{1,0:T(8,128)(2,1)S(1)} custom-call(bf16[128,12288]{1,0:T(8,128)(2,1)} %queries.1, bf16[128,512]{1,0:T(8,128)(2,1)} %latent.1, bf16[64,128]{1,0:T(8,128)(2,1)} %bitcast.1, bf16[64,2048]{1,0:T(8,128)(2,1)} %key_weight.1, bf16[64,2048]{1,0:T(8,128)(2,1)} %value_weight.1, s32[32]{0:T(128)} %lengths_in.1), custom_call_target="tpu_custom_call" | custom-call | tf_op jit(solution)/shard_map/pallas_call | solution.py:516
  56.4 1.3 %copy.8 = bf16[128,8192]{1,0:T(8,128)(2,1)} copy(bf16[128,8192]{1,0:T(8,128)(2,1)S(1)} %shard_map.64) | data formatting | bytes 4194304

commit v4 on v3

--- a/solution.py
+++ b/solution.py
@@ -15,6 +15,15 @@
 LOG2E = 1.4426950408889634
 
 MESH = pl.DeviceIdType.MESH
+
+
+PLAN = (
+    "r01", "lat", "q1", "z11", "b4", "own", "z21", "q2", "r02", "z41", "z12", "back", "z22",
+    "r03", "e3", "done", "rope", "give", "qx", "z42", "i3", "z13", "z23", "r04", "w0",
+    "relay", "z31", "y10", "y11", "y12", "y13", "w1", "pass", "row", "z32", "y20", "y21",
+    "y22", "y23", "w2", "y40", "y41", "y42", "in", "w4", "z33", "y30", "y31", "y32", "y33",
+    "w3",
+)
 
 
 def ring_order(pieces, wide, steps_of):
@@ -40,6 +49,8 @@
 def kernel(
     sizes, queries, latent, rope_keys, key_weight, value_weight, lengths_in, out,
     lat_all, rope_all, w, qbuf, kaug, vbuf, bias, obuf, lengths,
+    lat_ext, rope_ext, q_ext, kaug_ext, vbuf_ext, bias_ext, obuf_ext,
+    z_recv, y_recv, c_send, ext_sem, ext_send, qe_sem, qe_send, oe_send,
     len_sem, lat_sem, lat_send, w_own, w_recv, w_send, x_send, x_recv, q_sem, q_send, o_sem, o_send,
 ):
     n_seq, n_head, look, wide, chunk_heads = sizes
@@ -66,9 +77,15 @@
 
     after, before = at_place(place + 1), at_place(place - 1)
 
-    shown = head - (n_head - look)
-    gives = (shown >= 0) & (seq < n_seq - 1)
-    takes = (shown >= 0) & (seq > 0)
+    cols = (pieces, wide, half, look) == (5, 3, 4, 1)
+    z, y = seq // 2, seq % 2
+    inner = (z > 0) & (z < half - 1)
+    outer = jnp.logical_not(inner)
+    other, ally = seq + 1 - 2 * y, seq + 2 - 4 * (z % 2)
+
+    sides = sorted({(n_head - look + i) % 2 for i in range(look)})
+    helps = (core >= 0) if len(sides) > 1 else (core == sides[0])
+    gives, takes = helps & (seq < n_seq - 1), helps & (seq > 0)
 
     barrier = pltpu.get_barrier_semaphore()
 
@@ -79,6 +96,10 @@
     greet(before, head)
     for k in range(1, n_head):
         greet(seq, (head + k) % n_head)
+
+    if cols:
+        greet(other, head)
+        greet(ally, mate)
 
     @pl.when(gives)
     def _():
@@ -108,16 +129,21 @@
                 queries.at[:, q_cols(head, c)], qbuf.at[c, head], q_sem.at[c]
             ).start()
         for k in range(xs):
-            pltpu.make_async_copy(
+            mine_too = pltpu.make_async_copy(
                 queries.at[:, q_cols(owner(k, core), wide)],
                 qbuf.at[wide + k, core], q_sem.at[wide + k],
-            ).start()
+            )
+            if cols and k > 0:
+                pl.when(inner)(mine_too.start)
+            else:
+                mine_too.start()
 
     own_copies()
     pltpu.make_async_copy(lengths_in, lengths, len_sem).start()
     with jax.named_scope("barrier"):
         pl.semaphore_wait(
-            barrier, n_head + 1 + gives.astype(jnp.int32) + takes.astype(jnp.int32)
+            barrier,
+            n_head + 1 + 2 * cols + gives.astype(jnp.int32) + takes.astype(jnp.int32),
         )
 
     def lat_copies(index, slot, to, landing):
@@ -140,18 +166,15 @@
         sent = [lat_copies(k - 1, mine, (seq, owner(k, core)), mine) for k in range(1, xs)]
         return sent + [lat_copies(xs - 1, mine, (seq, mate), mine)]
 
-    def back_out():
-        return lat_copies(xs, mine, (seq + 1, head), shown)
-
     def lat_on(k):
         slot = look + owner(k, core)
-        return lat_copies(xs + k, slot, (seq, mate), slot)
-
-    def back_on(k):
-        return lat_copies(2 * xs + k - 1, shown, (seq, owner(k, core)), shown)
+        return lat_copies(xs + look + k - 1, slot, (seq, mate), slot)
+
+    def back_out(i):
+        return lat_copies(xs + i, n_head + i, (seq + 1, head), i)
 
     def back_mate(i):
-        return lat_copies(3 * xs - 1 + i, i, (seq, mate), i)
+        return lat_copies(2 * xs + look - 1 + i, i, (seq, mate), i)
 
     def back_side(i):
         return core == (n_head - look + i) % 2
@@ -232,25 +255,170 @@
             device_id=(seq, peer), device_id_type=MESH,
         )
 
+    def z_copy(c, t, origin, up):
+        block = w.at[c, 2 * origin + y]
+        return pltpu.make_async_remote_copy(
+            src_ref=block, dst_ref=block, send_sem=c_send.at[c // 3],
+            recv_sem=z_recv.at[c - 1, t - 1],
+            device_id=(seq + 2 * up, head), device_id_type=MESH,
+        )
+
+    def y_copy(c, t, origin):
+        block = w.at[c, 2 * origin + y]
+        return pltpu.make_async_remote_copy(
+            src_ref=block, dst_ref=block, send_sem=c_send.at[c // 3],
+            recv_sem=y_recv.at[c - 1, t],
+            device_id=(other, head), device_id_type=MESH,
+        )
+
+    def column_start(c):
+        if c == 4:
+            arrive(w.at[c, 0], x_recv.at[0])
+        pl.when(z <= (half - 3 if c == 4 else half - 2))(z_copy(c, 1, z, 1).start)
+        pl.when(z >= (2 if c == 4 else 1))(z_copy(c, 1, z, -1).start)
+        if c == 4:
+            pl.when(inner)(y_copy(c, 0, z).start)
+        else:
+            y_copy(c, 0, z).start()
+
+    def z_take(c, t):
+        one, two, sem = w.at[c, 0], w.at[c, pl.ds(0, 2)], z_recv.at[c - 1, t - 1]
+        far = z + 2 - 4 * (z // 2)
+
+        def first_inner():
+            arrive(two, sem)
+            pl.when(z <= (1 if c == 4 else half))(z_copy(c, 2, z - 1, 1).start)
+            pl.when(z >= (2 if c == 4 else 0))(z_copy(c, 2, z + 1, -1).start)
+            if c == 3:
+                y_copy(c, 1, half - 1 - z).start()
+            else:
+                y_copy(c, 1, z - 1).start()
+                y_copy(c, 1, z + 1).start()
+
+        def first_outer():
+            arrive(one, sem)
+            y_copy(c, 1, z + 1 - 2 * (z % 2)).start()
+
+        def second():
+            arrive(one, sem)
+            if c < 4:
+                pl.when(z == 1)(z_copy(c, 3, far, -1).start)
+                pl.when(z == 2)(z_copy(c, 3, far, 1).start)
+            y_copy(c, 2, far).start()
+
+        def third():
+            arrive(one, sem)
+            y_copy(c, 3, half - 1 - z).start()
+
+        if t == 1:
+            pl.when(inner)(first_inner)
+            if c < 4:
+                pl.when(outer)(first_outer)
+        elif t == 2 and c == 4:
+            pl.when(inner)(second)
+        elif t == 2:
+            second()
+        elif c < 4:
+            pl.when(outer)(third)
+
+    def y_take(c, t):
+        one, two, sem = w.at[c, 0], w.at[c, pl.ds(0, 2)], y_recv.at[c - 1, t]
+        if c == 3 and t == 0:
+            pl.when(inner)(lambda: arrive(one, sem))
+        elif c == 3:
+            arrive(one, sem)
+        elif t == 1:
+            pl.when(inner)(lambda: arrive(two, sem))
+            if c < 4:
+                pl.when(outer)(lambda: arrive(one, sem))
+        elif t == 3:
+            pl.when(outer)(lambda: arrive(one, sem))
+        elif c == 4:
+            pl.when(inner)(lambda: arrive(one, sem))
+        else:
+            arrive(one, sem)
+
+    def row_on():
+        block = w.at[3, other]
+        return pltpu.make_async_remote_copy(
+            src_ref=block, dst_ref=block, send_sem=c_send.at[1], recv_sem=y_recv.at[2, 3],
+            device_id=(ally, head), device_id_type=MESH,
+        )
+
+    def row_take():
+        arrive(w.at[3, 0], y_recv.at[2, 0])
+        row_on().start()
+
+    def ext_copies(index, sources, slot, to):
+        return [
+            pltpu.make_async_remote_copy(
+                src_ref=source, dst_ref=landing.at[slot],
+                send_sem=ext_send.at[index, part], recv_sem=ext_sem.at[slot, part],
+                device_id=to, device_id_type=MESH,
+            )
+            for part, (source, landing) in enumerate(zip(sources, (lat_ext, rope_ext)))
+        ]
+
+    def ext_wait(slot):
+        arrive(lat_ext.at[slot], ext_sem.at[slot, 0])
+        arrive(rope_ext.at[slot], ext_sem.at[slot, 1])
+
+    def ext_give_own():
+        start(ext_copies(0, (lat_all.at[mine], rope_all.at[mine]), 1 + core, (ally, head)))
+
+    def ext_give_back():
+        start(ext_copies(1, (lat_all.at[2 * x], rope_all.at[2 * x]), 0, (ally, head)))
+
+    def ext_relay():
+        ext_wait(1 + core)
+        start(ext_copies(0, (lat_ext.at[1 + core], rope_ext.at[1 + core]), 1 + core, (seq, mate)))
+
+    def ext_relay_back():
+        ext_wait(0)
+        start(ext_copies(1, (lat_ext.at[0], rope_ext.at[0]), 0, (seq, mate)))
+
+    def ext_done():
+        ext_wait(2 - core)
+        pl.when(core == 1)(lambda: ext_wait(0))
+
+    def ext_queries():
+        for side in range(2):
+            pltpu.make_async_remote_copy(
+                src_ref=queries.at[:, q_cols(owner(1, side), wide)], dst_ref=q_ext.at[core],
+                send_sem=qe_send, recv_sem=qe_sem,
+                device_id=(ally, 2 * x + side), device_id_type=MESH,
+            ).start()
+
+    def ext_out(tile):
+        return pltpu.make_async_remote_copy(
+            src_ref=obuf_ext.at[tile], dst_ref=out.at[:, o_cols(owner(1, core), wide)],
+            send_sem=oe_send, recv_sem=o_sem,
+            device_id=(ally, 2 * x + tile), device_id_type=MESH,
+        )
+
     order, holds = ring_order(pieces, wide, steps_of)
     arrive(w.at[pl.ds(0, wide + 1), 0], w_own)
     ring_send(*order[0])
-    ring_send(*order[1])
+    if cols:
+        column_start(1)
+        column_start(2)
+    else:
+        ring_send(*order[1])
     lat_wait(mine)
     start([copy for copies in lat_out() for copy in copies])
+    if cols:
+        x_copy(1, 0).start()
     start(q_copies(0))
-
-    @pl.when(gives)
-    def _():
-        start(back_out())
-
     for c in range(wide, pieces):
-        start(q_copies(c))
+        if cols and c > wide:
+            pl.when(inner)(lambda: start(q_copies(c)))
+        else:
+            start(q_copies(c))
 
     docs = lengths.shape[0]
-    first = seq * n_head * tok
-
-    def mask_tile(j, carry):
+
+    def mask_of(group, j):
+        first = group * n_head * tok
         q_place = first + j * tok + lax.broadcasted_iota(jnp.int32, (tok, 1), 0)
 
         def document(d, state):
@@ -262,12 +430,27 @@
         )
         k_place = first + (j - look) * tok + lax.broadcasted_iota(jnp.int32, (tok, span), 1)
         seen = (k_place >= begun) & (k_place <= q_place)
-        bias[j] = jnp.where(seen, 0.0, -jnp.inf)
+        return jnp.where(seen, 0.0, -jnp.inf)
+
+    def mask_tile(j, carry):
+        bias[j] = mask_of(seq, j)
+        return carry
+
+    def mask_ext(j, carry):
+        bias_ext[j] = mask_of(ally, 2 * x + j)
         return carry
 
     with jax.named_scope("mask"):
         pltpu.make_async_copy(lengths_in, lengths, len_sem).wait()
         lax.fori_loop(0, n_head, mask_tile, 0)
+        if cols:
+            @pl.when(inner)
+            def _():
+                lax.fori_loop(0, 2, mask_ext, 0)
+                for h in range(chunk_heads):
+                    vbuf_ext[:, (2 * h + 1) * VDIM:(2 * h + 2) * VDIM] = jnp.ones(
+                        ((look + 2) * tok, VDIM), jnp.bfloat16
+                    )
 
         @pl.when(seq == 0)
         def _():
@@ -284,21 +467,16 @@
             lat_wait(look + owner(k, core))
             start(lat_on(k))
 
+        for i in range(look):
+            @pl.when(back_side(i) & (seq < n_seq - 1))
+            def _():
+                start(back_out(i))
+
     def back_relay():
-        @pl.when(takes)
-        def _():
-            lat_wait(shown)
-            for k in range(1, xs):
-                start(back_on(k))
-
-    def back_relay_mate():
         for i in range(look):
             @pl.when(back_side(i) & (seq > 0))
             def _():
-                @pl.when(head != n_head - look + i)
-                def _():
-                    lat_wait(i)
-
+                lat_wait(i)
                 start(back_mate(i))
 
     def lat_done():
@@ -309,22 +487,29 @@
             def _():
                 lat_wait(i)
 
-    def rope_in():
+    def rope_in(ropes, augmented, count):
         first_half = lax.broadcasted_iota(jnp.int32, (tok, 2 * ROPE), 1) < ROPE
 
         def fill(slot, carry):
-            rope = rope_all[slot].astype(jnp.float32)
+            rope = ropes[slot].astype(jnp.float32)
             twice = jnp.concatenate([rope, rope], axis=0).T
             at = pl.ds(pl.multiple_of(slot * tok, tok), tok)
             for h in range(chunk_heads):
                 laid = jnp.where(first_half, twice, 0.0) if h % 2 == 0 else twice
-                kaug[h, at, NOPE:] = laid.astype(jnp.bfloat16)
+                augmented[h, at, NOPE:] = laid.astype(jnp.bfloat16)
             return carry
 
-        lax.fori_loop(0, slots, fill, 0)
-
-    def project(c):
-        first_slot, tiles = (0, slots) if c < wide else (2 * x, look + 2)
+        lax.fori_loop(0, count, fill, 0)
+
+    def rope_own():
+        rope_in(rope_all, kaug, slots)
+
+    own_refs = (lat_all, kaug, vbuf, bias, qbuf, obuf)
+    ext_refs = (lat_ext, kaug_ext, vbuf_ext, bias_ext, q_ext, obuf_ext)
+
+    def project(c, ext):
+        lat_all, kaug, vbuf = (ext_refs if ext else own_refs)[:3]
+        first_slot, tiles = (0, slots) if c < wide else (0 if ext else 2 * x, look + 2)
         parts = -(-tiles // 6)
         done = 0
         for part in range(parts):
@@ -362,15 +547,19 @@
 
     scale = LOG2E / math.sqrt(QK)
 
-    def attend(c, tiles, then):
+    def attend(c, tiles, then, ext):
+        _, kaug, vbuf, bias, queries_in, given_out = ext_refs if ext else own_refs
+        if not ext:
+            queries_in, given_out = qbuf.at[c], obuf.at[c]
+
         def places(tile):
-            place_of = tile if c < wide else 2 * x + tile
+            place_of = tile if c < wide or ext else 2 * x + tile
             return place_of, pl.ds(pl.multiple_of(place_of * tok, tok), span)
 
         def scores(tile, h):
             begin = (h // 2) * 2 * QK + (h % 2) * NOPE
             return lax.dot_general(
-                qbuf[c, tile, :, begin:begin + 2 * NOPE], kaug[h, places(tile)[1], :],
+                queries_in[tile, :, begin:begin + 2 * NOPE], kaug[h, places(tile)[1], :],
                 (((1,), (1,)), ((), ())), preferred_element_type=jnp.float32,
             )
 
@@ -385,7 +574,7 @@
                 preferred_element_type=jnp.float32,
             )
             given = (both[:, :VDIM] / both[:, VDIM:]).astype(jnp.bfloat16)
-            obuf[c, tile, :, h * VDIM:(h + 1) * VDIM] = given
+            given_out[tile, :, h * VDIM:(h + 1) * VDIM] = given
 
         items = [(tile, h) for tile in tiles for h in range(chunk_heads)]
         held = [scores(tile, h) for tile, h in items]
@@ -394,10 +583,10 @@
             expo[i] = weights(tile, held[i])
             if i > 0:
                 mix(*items[i - 1], expo.pop(i - 1))
-            if i == chunk_heads and c == last:
+            if i == chunk_heads and c == last and not ext:
                 then[0]()
         mix(*items[-1], expo.pop(len(items) - 1))
-        if c != last:
+        if c != last or ext:
             then[0]()
         then[1]()
 
@@ -405,7 +594,7 @@
         landed = qbuf.at[c] if c < wide else qbuf.at[c, pl.ds(0, 2)]
         pltpu.make_async_copy(landed, landed, q_sem.at[c]).wait()
 
-    last = order[-1][0]
+    last = wide if cols else order[-1][0]
 
     def work_on(c):
         tiles = n_head if c < wide else 2
@@ -421,75 +610,174 @@
                     q_in(c)
             with jax.named_scope(f"work{c}_{j}"):
                 if j == 0:
-                    project(c)
-                attend(c, [tile_at(c, j), tile_at(c, j + 1)], (o_copy(c, j).start, second_sent))
-
+                    project(c, False)
+                attend(c, [tile_at(c, j), tile_at(c, j + 1)], (o_copy(c, j).start, second_sent), False)
+
+        def ally_pair():
+            arrive(q_ext, qe_sem)
+            project(c, True)
+            attend(c, [0, 1], (ext_out(0).start, ext_out(1).start), True)
+
+        if cols and c > wide:
+            return [
+                (0.8, lambda: pl.when(inner)(lambda: pair(0))),
+                (0.8, lambda: pl.when(inner)(ally_pair)),
+            ]
         return [(0.8, functools.partial(pair, j)) for j in range(0, tiles, 2)]
 
-    chores = {
-        (0, 1): [lat_relay],
-        (1, 1): [back_relay] + [lambda c=c: start(q_copies(c)) for c in range(1, min(2, wide))]
-        + [lambda k=k: x_copy(k, 0).start() for k in range(1, xs)],
-        (0, 2): [back_relay_mate],
-        (1, 2): [lat_done, rope_in],
-    }
-    chores.setdefault((wide, 1), []).extend(
-        [lambda k=k: x_copy(k, 1).start() for k in range(1, xs)]
-        + [lambda c=c: start(q_copies(c)) for c in range(2, wide)]
-    )
-    unsent, waiting, taken = order[2:], [], set()
-    for c, t in order:
-        with jax.named_scope(f"ring{c}_{t}"):
-            ring_take(c, t)
-        taken.add((c, t))
-        while unsent:
-            ahead, step = unsent[0]
-            need = (ahead, step - 1) if step > 1 else holds.get(ahead)
-            if need is not None and need not in taken:
-                break
-            ring_send(*unsent.pop(0))
-        for chore in chores.get((c, t), []):
-            with jax.named_scope("chore"):
-                chore()
-        if t == steps_of(c):
-            waiting += work_on(c)
-        room = 1.8
-        while waiting and room > 0:
-            cost, step = waiting.pop(0)
+    def column_plan():
+        def only_inner(work):
+            return lambda: pl.when(inner)(work)
+
+        def only_outer(work):
+            return lambda: pl.when(outer)(work)
+
+        def ext_in():
+            ext_done()
+            rope_in(rope_ext, kaug_ext, look + 2)
+
+        def back():
+            pl.when(outer & (core == 0))(ext_give_back)
+
+        def relay_back():
+            pl.when(inner & (core == 0))(ext_relay_back)
+
+        steps = {"r": ring_step, "z": z_take, "y": y_take}
+        plan = PLAN
+        todo = {
+            "lat": lat_relay, "q1": lambda: start(q_copies(1)), "q2": lambda: start(q_copies(2)),
+            "qx": only_outer(ext_queries), "back": back_relay, "done": lat_done,
+            "rope": rope_own, "give": back, "own": only_outer(ext_give_own),
+            "e3": only_outer(lambda: column_start(3)),
+            "i3": only_inner(lambda: column_start(3)),
+            "row": only_outer(row_take), "relay": only_inner(ext_relay), "pass": relay_back,
+            "in": only_inner(ext_in),
+        }
+        waiting = []
+        for step in plan:
+            kind, rest = step[0], step[1:]
+            with jax.named_scope(step):
+                if step in todo:
+                    todo[step]()
+                elif kind == "b":
+                    column_start(int(rest))
+                elif kind == "w":
+                    waiting += work_on(int(rest))
+                else:
+                    steps[kind](int(rest[0]), int(rest[1]))
+            room = 1.8 if kind in "rzyw" else 0
+            while waiting and room > 0:
+                cost, work = waiting.pop(0)
+                work()
+                room -= cost
+        for _, work in waiting:
+            work()
+
+    def ring_step(c, t):
+        ring_take(c, t)
+        if t < half:
+            ring_send(c, t + 1)
+
+    def ring_plan():
+        chores = {
+            (0, 1): [lat_relay],
+            (1, 1): [lambda c=c: start(q_copies(c)) for c in range(1, min(2, wide))]
+            + [lambda k=k: x_copy(k, 0).start() for k in range(1, xs)],
+            (0, min(3, half - 1)): [back_relay],
+        }
+        chores.setdefault(order[order.index((0, half)) - 1], []).extend([lat_done, rope_own])
+        chores.setdefault((wide, 1), []).extend(
+            [lambda k=k: x_copy(k, 1).start() for k in range(1, xs)]
+            + [lambda c=c: start(q_copies(c)) for c in range(2, wide)]
+        )
+        unsent, waiting, taken = order[2:], [], set()
+        for c, t in order:
+            with jax.named_scope(f"ring{c}_{t}"):
+                ring_take(c, t)
+            taken.add((c, t))
+            while unsent:
+                ahead, step = unsent[0]
+                need = (ahead, step - 1) if step > 1 else holds.get(ahead)
+                if need is not None and need not in taken:
+                    break
+                ring_send(*unsent.pop(0))
+            for chore in chores.get((c, t), []):
+                with jax.named_scope("chore"):
+                    chore()
+            if t == steps_of(c):
+                waiting += work_on(c)
+            room = 1.8
+            while waiting and room > 0:
+                cost, step = waiting.pop(0)
+                step()
+                room -= cost
+        for _, step in waiting:
             step()
-            room -= cost
-    for _, step in waiting:
-        step()
+
+    if cols:
+        column_plan()
+    else:
+        ring_plan()
 
     with jax.named_scope("last"):
-        landed = out.at[:, pl.ds(0, (wide * (n_head - 1) + xs) * cw)]
-        pltpu.make_async_copy(landed, landed, o_sem).wait()
+        def outs(many):
+            arrive(out.at[:, pl.ds(0, (wide * (n_head - 1) + many) * cw)], o_sem)
+
+        if cols:
+            pl.when(inner)(lambda: outs(xs))
+            pl.when(outer)(lambda: outs(xs + 1))
+        else:
+            outs(xs)
 
     with jax.named_scope("sends"):
         arrive(obuf.at[pl.ds(0, wide), pl.ds(0, n_head - 1)], o_send.at[0])
-        arrive(obuf.at[pl.ds(wide, xs), pl.ds(0, 1)], o_send.at[1])
         arrive(qbuf.at[pl.ds(0, wide), pl.ds(0, n_head - 1)], q_send.at[0])
-        arrive(qbuf.at[pl.ds(wide, xs), pl.ds(0, 1)], q_send.at[1])
-        arrive(w.at[pl.ds(0, wide + 1), pl.ds(0, n_seq - 1)], w_send.at[0])
-        arrive(w.at[pl.ds(wide + 1, xs - 1), pl.ds(0, n_seq - 2)], w_send.at[1])
-        for k in range(1, xs):
-            arrive(w.at[wide, pl.ds(0, 2)], x_send.at[k - 1])
+
+        def local_sent(many):
+            arrive(obuf.at[pl.ds(wide, many), pl.ds(0, 1)], o_send.at[1])
+            arrive(qbuf.at[pl.ds(wide, many), pl.ds(0, 1)], q_send.at[1])
+
+        if cols:
+            arrive(w.at[0, pl.ds(0, n_seq - 1)], w_send.at[0])
+            arrive(w.at[0, 0], x_send.at[0])
+
+            def inner_sent():
+                local_sent(2)
+                arrive(w.at[pl.ds(0, 3), pl.ds(0, 6)], c_send.at[0])
+                arrive(w.at[pl.ds(0, 2), pl.ds(0, 7)], c_send.at[1])
+                arrive(obuf_ext, oe_send)
+
+            def outer_sent():
+                local_sent(1)
+                arrive(w.at[pl.ds(0, 2), pl.ds(0, 5)], c_send.at[0])
+                arrive(w.at[0, pl.ds(0, 7)], c_send.at[1])
+                arrive(q_ext, qe_send)
+
+            pl.when(inner)(inner_sent)
+            pl.when(outer)(outer_sent)
+
+            def ext_sent(index):
+                arrive(lat_ext.at[0], ext_send.at[index, 0])
+                arrive(rope_ext.at[0], ext_send.at[index, 1])
+
+            ext_sent(0)
+            pl.when(core == 0)(lambda: ext_sent(1))
+        else:
+            local_sent(xs)
+            arrive(w.at[pl.ds(0, wide + 1), pl.ds(0, n_seq - 1)], w_send.at[0])
+            arrive(w.at[pl.ds(wide + 1, xs - 1), pl.ds(0, n_seq - 2)], w_send.at[1])
+            for k in range(1, xs):
+                arrive(w.at[wide, pl.ds(0, 2)], x_send.at[k - 1])
         for copies in lat_out() + [lat_on(k) for k in range(1, xs)]:
             for copy in copies:
                 copy.wait_send()
 
-        @pl.when(gives)
-        def _():
-            for copy in back_out():
-                copy.wait_send()
-
-        @pl.when(takes)
-        def _():
-            for k in range(1, xs):
-                for copy in back_on(k):
+        for i in range(look):
+            @pl.when(back_side(i) & (seq < n_seq - 1))
+            def _():
+                for copy in back_out(i):
                     copy.wait_send()
 
-        for i in range(look):
             @pl.when(back_side(i) & (seq > 0))
             def _():
                 for copy in back_mate(i):
@@ -528,11 +816,26 @@
             pltpu.VMEM((n_head, tok, span), jnp.float32),
             pltpu.VMEM((pieces, n_head, tok, cw), bf16),
             pltpu.SMEM((docs,), jnp.int32),
+            pltpu.VMEM((look + 2, tok, rank), bf16),
+            pltpu.VMEM((look + 2, ROPE, tok), bf16),
+            pltpu.VMEM((2, tok, qw), bf16),
+            pltpu.VMEM((chunk_heads, (look + 2) * tok, 2 * NOPE), bf16),
+            pltpu.VMEM(((look + 2) * tok, 2 * cw), bf16),
+            pltpu.VMEM((2, tok, span), jnp.float32),
+            pltpu.VMEM((2, tok, cw), bf16),
+            dma((4, 3)),
+            dma((4, 4)),
+            dma((2,)),
+            dma((look + 2, 2)),
+            dma((2, 2)),
+            dma,
+            dma,
+            dma,
             dma,
             dma((slots, 2)),
-            dma((3 * xs - 1 + look, 2)),
+            dma((2 * xs - 1 + 2 * look, 2)),
             dma,
-            dma((pieces, half)),
+            dma((1 if (pieces, wide, half, look) == (5, 3, 4, 1) else pieces, half)),
             dma((2,)),
             dma((xs - 1,)),
             dma((xs - 1,)),

time: 58.2 us -> 55.2 us (0.948)
  Pallas kernels: 56.4 us -> 53.7 us
    pallas_call x1, Pallas kernels: 56.4 us -> 53.7 us  [shards(): pl.pallas_call(functools.partial(kernel, (n_seq, n_head, look, wide, chun...]
where the time goes in v4:
time: 55.2 us; the launch traced here: 55 us
  Pallas kernels  53.7 us (97%)
  local copies, waits for them, and re-layouts  1.32 us (2%)
    pallas_call x1, Pallas kernels, shards(): pl.pallas_call(functools.partial(kernel, (n_seq, n_head, look, wide, chun...  53.7 us
    unnamed x1, local copies, waits for them, and re-layouts  1.32 us

profile of v4, /device:TPU:1, one launch (start us, length us, event | category | flops | bytes accessed | tf_op | source)
XLA Modules:
  0.0 55.0 jit_solution(17509811528306520370)
XLA Ops:
  0.0 53.7 %shard_map.64 = bf16[128,8192]{1,0:T(8,128)(2,1)S(1)} custom-call(bf16[128,12288]{1,0:T(8,128)(2,1)} %queries.1, bf16[128,512]{1,0:T(8,128)(2,1)} %latent.1, bf16[64,128]{1,0:T(8,128)(2,1)} %bitcast.1, bf16[64,2048]{1,0:T(8,128)(2,1)} %key_weight.1, bf16[64,2048]{1,0:T(8,128)(2,1)} %value_weight.1, s32[32]{0:T(128)} %lengths_in.1), custom_call_target="tpu_custom_call" | custom-call | tf_op jit(solution)/shard_map/pallas_call | solution.py:804
  53.7 1.3 %copy.8 = bf16[128,8192]{1,0:T(8,128)(2,1)} copy(bf16[128,8192]{1,0:T(8,128)(2,1)S(1)} %shard_map.64) | data formatting | bytes 4194304

commit v5 on v4

--- a/solution.py
+++ b/solution.py
@@ -20,9 +20,8 @@
 PLAN = (
     "r01", "lat", "q1", "z11", "b4", "own", "z21", "q2", "r02", "z41", "z12", "back", "z22",
     "r03", "e3", "done", "rope", "give", "qx", "z42", "i3", "z13", "z23", "r04", "w0",
-    "relay", "z31", "y10", "y11", "y12", "y13", "w1", "pass", "row", "z32", "y20", "y21",
-    "y22", "y23", "w2", "y40", "y41", "y42", "in", "w4", "z33", "y30", "y31", "y32", "y33",
-    "w3",
+    "relay", "z31", "y1", "w1", "pass", "row", "z32", "y2", "w2", "y4", "in", "w4", "z33",
+    "y3", "w3",
 )
 
 
@@ -163,18 +162,18 @@
     mine = look + head
 
     def lat_out():
-        sent = [lat_copies(k - 1, mine, (seq, owner(k, core)), mine) for k in range(1, xs)]
-        return sent + [lat_copies(xs - 1, mine, (seq, mate), mine)]
+        sent = [lat_copies(0, mine, (seq, owner(k, core)), mine) for k in range(1, xs)]
+        return sent + [lat_copies(0, mine, (seq, mate), mine)]
 
     def lat_on(k):
         slot = look + owner(k, core)
-        return lat_copies(xs + look + k - 1, slot, (seq, mate), slot)
+        return lat_copies(0, slot, (seq, mate), slot)
 
     def back_out(i):
-        return lat_copies(xs + i, n_head + i, (seq + 1, head), i)
+        return lat_copies(1 + i, n_head + i, (seq + 1, head), i)
 
     def back_mate(i):
-        return lat_copies(2 * xs + look - 1 + i, i, (seq, mate), i)
+        return lat_copies(1 + look + i, i, (seq, mate), i)
 
     def back_side(i):
         return core == (n_head - look + i) % 2
@@ -267,7 +266,7 @@
         block = w.at[c, 2 * origin + y]
         return pltpu.make_async_remote_copy(
             src_ref=block, dst_ref=block, send_sem=c_send.at[c // 3],
-            recv_sem=y_recv.at[c - 1, t],
+            recv_sem=y_recv.at[4 if c == 3 and t == 0 else c - 1],
             device_id=(other, head), device_id_type=MESH,
         )
 
@@ -321,32 +320,27 @@
         elif c < 4:
             pl.when(outer)(third)
 
-    def y_take(c, t):
-        one, two, sem = w.at[c, 0], w.at[c, pl.ds(0, 2)], y_recv.at[c - 1, t]
-        if c == 3 and t == 0:
-            pl.when(inner)(lambda: arrive(one, sem))
-        elif c == 3:
-            arrive(one, sem)
-        elif t == 1:
-            pl.when(inner)(lambda: arrive(two, sem))
-            if c < 4:
-                pl.when(outer)(lambda: arrive(one, sem))
-        elif t == 3:
-            pl.when(outer)(lambda: arrive(one, sem))
+    def y_take(c):
+        def whole():
+            arrive(w.at[c, pl.ds(0, 4)], y_recv.at[c - 1])
+
+        if c == 3:
+            pl.when(inner)(lambda: arrive(w.at[c, 0], y_recv.at[4]))
+            arrive(w.at[c, pl.ds(0, 3)], y_recv.at[c - 1])
         elif c == 4:
-            pl.when(inner)(lambda: arrive(one, sem))
+            pl.when(inner)(whole)
         else:
-            arrive(one, sem)
+            whole()
 
     def row_on():
         block = w.at[3, other]
         return pltpu.make_async_remote_copy(
-            src_ref=block, dst_ref=block, send_sem=c_send.at[1], recv_sem=y_recv.at[2, 3],
+            src_ref=block, dst_ref=block, send_sem=c_send.at[1], recv_sem=y_recv.at[2],
             device_id=(ally, head), device_id_type=MESH,
         )
 
     def row_take():
-        arrive(w.at[3, 0], y_recv.at[2, 0])
+        arrive(w.at[3, 0], y_recv.at[4])
         row_on().start()
 
     def ext_copies(index, sources, slot, to):
@@ -398,16 +392,16 @@
 
     order, holds = ring_order(pieces, wide, steps_of)
     arrive(w.at[pl.ds(0, wide + 1), 0], w_own)
+    lat_wait(mine)
+    start([copy for copies in lat_out() for copy in copies])
+    if cols:
+        x_copy(1, 0).start()
     ring_send(*order[0])
     if cols:
         column_start(1)
         column_start(2)
     else:
         ring_send(*order[1])
-    lat_wait(mine)
-    start([copy for copies in lat_out() for copy in copies])
-    if cols:
-        x_copy(1, 0).start()
     start(q_copies(0))
     for c in range(wide, pieces):
         if cols and c > wide:
@@ -664,7 +658,7 @@
                 elif kind == "w":
                     waiting += work_on(int(rest))
                 else:
-                    steps[kind](int(rest[0]), int(rest[1]))
+                    steps[kind](*map(int, rest))
             room = 1.8 if kind in "rzyw" else 0
             while waiting and room > 0:
                 cost, work = waiting.pop(0)
@@ -768,9 +762,8 @@
             arrive(w.at[pl.ds(wide + 1, xs - 1), pl.ds(0, n_seq - 2)], w_send.at[1])
             for k in range(1, xs):
                 arrive(w.at[wide, pl.ds(0, 2)], x_send.at[k - 1])
-        for copies in lat_out() + [lat_on(k) for k in range(1, xs)]:
-            for copy in copies:
-                copy.wait_send()
+        arrive(lat_all.at[pl.ds(0, 2 * xs - 1)], lat_send.at[0, 0])
+        arrive(rope_all.at[pl.ds(0, 2 * xs - 1)], lat_send.at[0, 1])
 
         for i in range(look):
             @pl.when(back_side(i) & (seq < n_seq - 1))
@@ -824,7 +817,7 @@
             pltpu.VMEM((2, tok, span), jnp.float32),
             pltpu.VMEM((2, tok, cw), bf16),
             dma((4, 3)),
-            dma((4, 4)),
+            dma((5,)),
             dma((2,)),
             dma((look + 2, 2)),
             dma((2, 2)),
@@ -833,7 +826,7 @@
             dma,
             dma,
             dma((slots, 2)),
-            dma((2 * xs - 1 + 2 * look, 2)),
+            dma((1 + 2 * look, 2)),
             dma,
             dma((1 if (pieces, wide, half, look) == (5, 3, 4, 1) else pieces, half)),
             dma((2,)),

time: 55.2 us -> 55 us (level)
  no operation moved by 1% of the time
where the time goes in v5:
time: 55 us; the launch traced here: 54.9 us
  Pallas kernels  53.6 us (97%)
  local copies, waits for them, and re-layouts  1.32 us (2%)
    pallas_call x1, Pallas kernels, shards(): pl.pallas_call(functools.partial(kernel, (n_seq, n_head, look, wide, chun...  53.6 us
    unnamed x1, local copies, waits for them, and re-layouts  1.32 us

profile of v5, /device:TPU:1, one launch (start us, length us, event | category | flops | bytes accessed | tf_op | source)
XLA Modules:
  0.0 54.9 jit_solution(16751251619770137905)
XLA Ops:
  0.0 53.6 %shard_map.64 = bf16[128,8192]{1,0:T(8,128)(2,1)S(1)} custom-call(bf16[128,12288]{1,0:T(8,128)(2,1)} %queries.1, bf16[128,512]{1,0:T(8,128)(2,1)} %latent.1, bf16[64,128]{1,0:T(8,128)(2,1)} %bitcast.1, bf16[64,2048]{1,0:T(8,128)(2,1)} %key_weight.1, bf16[64,2048]{1,0:T(8,128)(2,1)} %value_weight.1, s32[32]{0:T(128)} %lengths_in.1), custom_call_target="tpu_custom_call" | custom-call | tf_op jit(solution)/shard_map/pallas_call | solution.py:797
  53.6 1.3 %copy.8 = bf16[128,8192]{1,0:T(8,128)(2,1)} copy(bf16[128,8192]{1,0:T(8,128)(2,1)S(1)} %shard_map.64) | data formatting | bytes 4194304

commit v6 on v5

--- a/solution.py
+++ b/solution.py
@@ -47,8 +47,8 @@
 
 def kernel(
     sizes, queries, latent, rope_keys, key_weight, value_weight, lengths_in, out,
-    lat_all, rope_all, w, qbuf, kaug, vbuf, bias, obuf, lengths,
-    lat_ext, rope_ext, q_ext, kaug_ext, vbuf_ext, bias_ext, obuf_ext,
+    lat_all, w, qbuf, kaug, vbuf, bias, obuf, lengths,
+    lat_ext, q_ext, kaug_ext, vbuf_ext, bias_ext, obuf_ext,
     z_recv, y_recv, c_send, ext_sem, ext_send, qe_sem, qe_send, oe_send,
     len_sem, lat_sem, lat_send, w_own, w_recv, w_send, x_send, x_recv, q_sem, q_send, o_sem, o_send,
 ):
@@ -57,6 +57,8 @@
     half = n_seq // 2
     xs = n_head // 2
     slots = look + n_head
+    folds = rank // tok
+    fold_rows = ROPE // folds
     span = (look + 1) * tok
     cw = chunk_heads * NOPE
     qw = chunk_heads * QK
@@ -121,8 +123,12 @@
                     source.at[:, pl.ds(c * cw, cw)], w.at[c, seq, kv], w_own
                 ).start()
         mine = look + head
-        pltpu.make_async_copy(latent, lat_all.at[mine], lat_sem.at[mine, 0]).start()
-        pltpu.make_async_copy(rope_keys, rope_all.at[mine], lat_sem.at[mine, 1]).start()
+        pltpu.make_async_copy(latent, lat_all.at[mine, pl.ds(0, tok)], lat_sem.at[mine]).start()
+        for a in range(folds):
+            pltpu.make_async_copy(
+                rope_keys.at[pl.ds(a * fold_rows, fold_rows)],
+                lat_all.at[mine, pl.ds(tok, fold_rows), pl.ds(a * tok, tok)], lat_sem.at[mine],
+            ).start()
         for c in range(wide):
             pltpu.make_async_copy(
                 queries.at[:, q_cols(head, c)], qbuf.at[c, head], q_sem.at[c]
@@ -148,16 +154,14 @@
     def lat_copies(index, slot, to, landing):
         return [
             pltpu.make_async_remote_copy(
-                src_ref=held.at[slot], dst_ref=held.at[landing],
-                send_sem=lat_send.at[index, part], recv_sem=lat_sem.at[landing, part],
+                src_ref=lat_all.at[slot], dst_ref=lat_all.at[landing],
+                send_sem=lat_send.at[index], recv_sem=lat_sem.at[landing],
                 device_id=to, device_id_type=MESH,
             )
-            for part, held in enumerate((lat_all, rope_all))
         ]
 
     def lat_wait(slot):
-        for part, held in enumerate((lat_all, rope_all)):
-            pltpu.make_async_copy(held.at[slot], held.at[slot], lat_sem.at[slot, part]).wait()
+        pltpu.make_async_copy(lat_all.at[slot], lat_all.at[slot], lat_sem.at[slot]).wait()
 
     mine = look + head
 
@@ -343,33 +347,31 @@
         arrive(w.at[3, 0], y_recv.at[4])
         row_on().start()
 
-    def ext_copies(index, sources, slot, to):
+    def ext_copies(index, source, slot, to):
         return [
             pltpu.make_async_remote_copy(
-                src_ref=source, dst_ref=landing.at[slot],
-                send_sem=ext_send.at[index, part], recv_sem=ext_sem.at[slot, part],
+                src_ref=source, dst_ref=lat_ext.at[slot],
+                send_sem=ext_send.at[index], recv_sem=ext_sem.at[slot],
                 device_id=to, device_id_type=MESH,
             )
-            for part, (source, landing) in enumerate(zip(sources, (lat_ext, rope_ext)))
         ]
 
     def ext_wait(slot):
-        arrive(lat_ext.at[slot], ext_sem.at[slot, 0])
-        arrive(rope_ext.at[slot], ext_sem.at[slot, 1])
+        arrive(lat_ext.at[slot], ext_sem.at[slot])
 
     def ext_give_own():
-        start(ext_copies(0, (lat_all.at[mine], rope_all.at[mine]), 1 + core, (ally, head)))
+        start(ext_copies(0, lat_all.at[mine], 1 + core, (ally, head)))
 
     def ext_give_back():
-        start(ext_copies(1, (lat_all.at[2 * x], rope_all.at[2 * x]), 0, (ally, head)))
+        start(ext_copies(1, lat_all.at[2 * x], 0, (ally, head)))
 
     def ext_relay():
         ext_wait(1 + core)
-        start(ext_copies(0, (lat_ext.at[1 + core], rope_ext.at[1 + core]), 1 + core, (seq, mate)))
+        start(ext_copies(0, lat_ext.at[1 + core], 1 + core, (seq, mate)))
 
     def ext_relay_back():
         ext_wait(0)
-        start(ext_copies(1, (lat_ext.at[0], rope_ext.at[0]), 0, (seq, mate)))
+        start(ext_copies(1, lat_ext.at[0], 0, (seq, mate)))
 
     def ext_done():
         ext_wait(2 - core)
@@ -448,8 +450,7 @@
 
         @pl.when(seq == 0)
         def _():
-            lat_all[:look] = jnp.zeros((look, tok, rank), jnp.bfloat16)
-            rope_all[:look] = jnp.zeros((look, ROPE, tok), jnp.bfloat16)
+            lat_all[:look] = jnp.zeros((look, tok + fold_rows, rank), jnp.bfloat16)
 
         for h in range(chunk_heads):
             vbuf[:, (2 * h + 1) * VDIM:(2 * h + 2) * VDIM] = jnp.ones(
@@ -481,11 +482,14 @@
             def _():
                 lat_wait(i)
 
-    def rope_in(ropes, augmented, count):
+    def rope_in(held, augmented, count):
         first_half = lax.broadcasted_iota(jnp.int32, (tok, 2 * ROPE), 1) < ROPE
 
         def fill(slot, carry):
-            rope = ropes[slot].astype(jnp.float32)
+            rope = jnp.concatenate(
+                [held[slot, tok:, a * tok:(a + 1) * tok].astype(jnp.float32) for a in range(folds)],
+                axis=0,
+            )
             twice = jnp.concatenate([rope, rope], axis=0).T
             at = pl.ds(pl.multiple_of(slot * tok, tok), tok)
             for h in range(chunk_heads):
@@ -496,7 +500,7 @@
         lax.fori_loop(0, count, fill, 0)
 
     def rope_own():
-        rope_in(rope_all, kaug, slots)
+        rope_in(lat_all, kaug, slots)
 
     own_refs = (lat_all, kaug, vbuf, bias, qbuf, obuf)
     ext_refs = (lat_ext, kaug_ext, vbuf_ext, bias_ext, q_ext, obuf_ext)
@@ -512,7 +516,7 @@
             done += many
             block = many * tok
             at = pl.ds(pl.multiple_of(slot * tok, tok), block)
-            lat = lat_all[pl.ds(slot, many)].reshape(block, rank)
+            lat = lat_all[pl.ds(slot, many), :tok].reshape(block, rank)
             low = lax.broadcasted_iota(jnp.int32, (block, NOPE), 1) < ROPE
 
             def up(kv, pair):
@@ -628,7 +632,7 @@
 
         def ext_in():
             ext_done()
-            rope_in(rope_ext, kaug_ext, look + 2)
+            rope_in(lat_ext, kaug_ext, look + 2)
 
         def back():
             pl.when(outer & (core == 0))(ext_give_back)
@@ -751,8 +755,7 @@
             pl.when(outer)(outer_sent)
 
             def ext_sent(index):
-                arrive(lat_ext.at[0], ext_send.at[index, 0])
-                arrive(rope_ext.at[0], ext_send.at[index, 1])
+                arrive(lat_ext.at[0], ext_send.at[index])
 
             ext_sent(0)
             pl.when(core == 0)(lambda: ext_sent(1))
@@ -762,8 +765,7 @@
             arrive(w.at[pl.ds(wide + 1, xs - 1), pl.ds(0, n_seq - 2)], w_send.at[1])
             for k in range(1, xs):
                 arrive(w.at[wide, pl.ds(0, 2)], x_send.at[k - 1])
-        arrive(lat_all.at[pl.ds(0, 2 * xs - 1)], lat_send.at[0, 0])
-        arrive(rope_all.at[pl.ds(0, 2 * xs - 1)], lat_send.at[0, 1])
+        arrive(lat_all.at[pl.ds(0, 2 * xs - 1)], lat_send.at[0])
 
         for i in range(look):
             @pl.when(back_side(i) & (seq < n_seq - 1))
@@ -800,8 +802,7 @@
         in_specs=[anywhere] * 6,
         out_specs=pl.BlockSpec(memory_space=pltpu.VMEM),
         scratch_shapes=[
-            pltpu.VMEM((slots, tok, rank), bf16),
-            pltpu.VMEM((slots, ROPE, tok), bf16),
+            pltpu.VMEM((slots, tok + ROPE * tok // rank, rank), bf16),
             pltpu.VMEM((pieces, n_seq, 2, rows, cw), bf16),
             pltpu.VMEM((pieces, n_head, tok, qw), bf16),
             pltpu.VMEM((chunk_heads, slots * tok, 2 * NOPE), bf16),
@@ -809,8 +810,7 @@
             pltpu.VMEM((n_head, tok, span), jnp.float32),
             pltpu.VMEM((pieces, n_head, tok, cw), bf16),
             pltpu.SMEM((docs,), jnp.int32),
-            pltpu.VMEM((look + 2, tok, rank), bf16),
-            pltpu.VMEM((look + 2, ROPE, tok), bf16),
+            pltpu.VMEM((look + 2, tok + ROPE * tok // rank, rank), bf16),
             pltpu.VMEM((2, tok, qw), bf16),
             pltpu.VMEM((chunk_heads, (look + 2) * tok, 2 * NOPE), bf16),
             pltpu.VMEM(((look + 2) * tok, 2 * cw), bf16),
@@ -819,14 +819,14 @@
             dma((4, 3)),
             dma((5,)),
             dma((2,)),
-            dma((look + 2, 2)),
-            dma((2, 2)),
+            dma((look + 2,)),
+            dma((2,)),
             dma,
             dma,
             dma,
             dma,
-            dma((slots, 2)),
-            dma((1 + 2 * look, 2)),
+            dma((slots,)),
+            dma((1 + 2 * look,)),
             dma,
             dma((1 if (pieces, wide, half, look) == (5, 3, 4, 1) else pieces, half)),
             dma((2,)),

time: 55 us -> 54.9 us (level)
  no operation moved by 1% of the time
where the time goes in v6:
time: 54.9 us; the launch traced here: 54.8 us
  Pallas kernels  53.5 us (97%)
  local copies, waits for them, and re-layouts  1.32 us (2%)
    pallas_call x1, Pallas kernels, shards(): pl.pallas_call(functools.partial(kernel, (n_seq, n_head, look, wide, chun...  53.5 us
    unnamed x1, local copies, waits for them, and re-layouts  1.32 us

profile of v6, /device:TPU:1, one launch (start us, length us, event | category | flops | bytes accessed | tf_op | source)
XLA Modules:
  0.0 54.8 jit_solution(2151952055570642636)
XLA Ops:
  0.0 53.5 %shard_map.64 = bf16[128,8192]{1,0:T(8,128)(2,1)S(1)} custom-call(bf16[128,12288]{1,0:T(8,128)(2,1)} %queries.1, bf16[128,512]{1,0:T(8,128)(2,1)} %latent.1, bf16[64,128]{1,0:T(8,128)(2,1)} %bitcast.1, bf16[64,2048]{1,0:T(8,128)(2,1)} %key_weight.1, bf16[64,2048]{1,0:T(8,128)(2,1)} %value_weight.1, s32[32]{0:T(128)} %lengths_in.1), custom_call_target="tpu_custom_call" | custom-call | tf_op jit(solution)/shard_map/pallas_call | solution.py:799
  53.5 1.3 %copy.8 = bf16[128,8192]{1,0:T(8,128)(2,1)} copy(bf16[128,8192]{1,0:T(8,128)(2,1)S(1)} %shard_map.64) | data formatting | bytes 4194304

commit v7 on v6

--- a/solution.py
+++ b/solution.py
@@ -393,9 +393,9 @@
         )
 
     order, holds = ring_order(pieces, wide, steps_of)
-    arrive(w.at[pl.ds(0, wide + 1), 0], w_own)
     lat_wait(mine)
     start([copy for copies in lat_out() for copy in copies])
+    arrive(w.at[pl.ds(0, wide + 1), 0], w_own)
     if cols:
         x_copy(1, 0).start()
     ring_send(*order[0])

time: 54.9 us -> 54.9 us (level)
  no operation moved by 1% of the time
where the time goes in v7:
time: 54.9 us; the launch traced here: 54.8 us
  Pallas kernels  53.4 us (97%)
  local copies, waits for them, and re-layouts  1.32 us (2%)
    pallas_call x1, Pallas kernels, shards(): pl.pallas_call(functools.partial(kernel, (n_seq, n_head, look, wide, chun...  53.4 us
    unnamed x1, local copies, waits for them, and re-layouts  1.32 us

profile of v7, /device:TPU:1, one launch (start us, length us, event | category | flops | bytes accessed | tf_op | source)
XLA Modules:
  0.0 54.8 jit_solution(12360315072667832493)
XLA Ops:
  0.0 53.4 %shard_map.64 = bf16[128,8192]{1,0:T(8,128)(2,1)S(1)} custom-call(bf16[128,12288]{1,0:T(8,128)(2,1)} %queries.1, bf16[128,512]{1,0:T(8,128)(2,1)} %latent.1, bf16[64,128]{1,0:T(8,128)(2,1)} %bitcast.1, bf16[64,2048]{1,0:T(8,128)(2,1)} %key_weight.1, bf16[64,2048]{1,0:T(8,128)(2,1)} %value_weight.1, s32[32]{0:T(128)} %lengths_in.1), custom_call_target="tpu_custom_call" | custom-call | tf_op jit(solution)/shard_map/pallas_call | solution.py:799
  53.5 1.3 %copy.8 = bf16[128,8192]{1,0:T(8,128)(2,1)} copy(bf16[128,8192]{1,0:T(8,128)(2,1)S(1)} %shard_map.64) | data formatting | bytes 4194304
